TPU v7x, 16 devices: a 4x2x1 block of a 4x4x8 slice. The times are simulated.
16 devices in a mesh: data: 2 (over y, z), seq: 8 (over x, core).
Axes of the slice: x: 4, y: 2, z: 1, core: 2. Of those that a mesh axis runs over, the one named last changes fastest.
The devices are a block of a 4x4x8 slice.
Arguments:
- x_in: bfloat16 [12, 2048, 2048], P(None, ('data', 'seq')), parts along dimension 1
- positions: int32 [2048], P(('data', 'seq')), parts along dimension 0
- w_query: bfloat16 [3, 2048, 24, 128], replicated
- w_key: bfloat16 [3, 2048, 24, 128], replicated
- w_value: bfloat16 [3, 2048, 24, 128], replicated
- w_out: bfloat16 [3, 24, 128, 2048], replicated
- w_up: bfloat16 [3, 2048, 8192], replicated
- w_down: bfloat16 [3, 8192, 2048], replicated
- g_attn: float32 [3, 2048], replicated
- g_mlp: float32 [3, 2048], replicated
Outputs:
- output: bfloat16 [12, 2048, 2048], P(None, ('data', 'seq')), parts along dimension 1
There are 2 independent parts. A program takes and returns all parts, laid end to end along the dimension named above; an argument that names none is the same for every part.
All inputs are finite; a program needn't handle non-finite values.
Results may differ from a plain program's by a relative error of at most 0.0147716.
Values are sent between devices in bfloat16 or wider.
A program may use at most 768 MiB of HBM per device.

v0:
```python
import jax
import jax.numpy as jnp
from jax import lax
from jax.sharding import PartitionSpec as P

ROPE_BASE = 10000.0
NORM_EPS = 1e-6


def rms_norm(x_act, gain_vec):
    x_f32 = x_act.astype(jnp.float32)
    mean_sq = jnp.mean(x_f32 * x_f32, axis=-1, keepdims=True)
    return (x_f32 * lax.rsqrt(mean_sq + NORM_EPS) * gain_vec).astype(jnp.bfloat16)


def rope_tables(positions, head_dim):
    inv_freq = ROPE_BASE ** (-jnp.arange(head_dim // 2, dtype=jnp.float32) * (2.0 / head_dim))
    angles = positions.astype(jnp.float32)[..., None] * inv_freq
    return jnp.cos(angles), jnp.sin(angles)


def apply_rope(proj_f32, cos_t, sin_t):
    half_dim = proj_f32.shape[-1] // 2
    x_first = proj_f32[..., :half_dim]
    x_second = proj_f32[..., half_dim:]
    cos_b = cos_t[..., None, :]
    sin_b = sin_t[..., None, :]
    return jnp.concatenate([x_first * cos_b - x_second * sin_b, x_second * cos_b + x_first * sin_b], axis=-1).astype(jnp.bfloat16)


def causal_attention(q_heads, k_heads, v_heads, q_offset, q_block):
    n_batch, q_len, kv_heads, groups, head_dim = q_heads.shape
    key_len = k_heads.shape[1]
    n_blocks = q_len // q_block
    att_scale = head_dim ** -0.5
    key_pos = jnp.arange(key_len)

    def one_block(blk_idx):
        blk_start = blk_idx * q_block
        q_blk = lax.dynamic_slice_in_dim(q_heads, blk_start, q_block, axis=1)
        scores = jnp.einsum("bqkgd,bskd->bkgqs", q_blk, k_heads, preferred_element_type=jnp.float32) * att_scale
        query_pos = q_offset + blk_start + jnp.arange(q_block)
        scores = jnp.where(key_pos[None, :] <= query_pos[:, None], scores, -1e30)
        row_max = jnp.max(scores, axis=-1, keepdims=True)
        exp_f32 = jnp.exp(scores - row_max)
        row_sum = jnp.sum(exp_f32, axis=-1)
        weighted = jnp.einsum("bkgqs,bskd->bqkgd", exp_f32.astype(jnp.bfloat16), v_heads, preferred_element_type=jnp.float32)
        return (weighted / jnp.transpose(row_sum, (0, 3, 1, 2))[..., None]).astype(jnp.bfloat16)

    blocks = lax.map(one_block, jnp.arange(n_blocks))
    return jnp.moveaxis(blocks, 0, 1).reshape(n_batch, q_len, kv_heads * groups, head_dim)


def layer_step(hidden, cos_t, sin_t, w_query, w_key, w_value, w_out, w_up, w_down, gain_attn, gain_mlp):
    normed = rms_norm(hidden, gain_attn)
    q_loc = apply_rope(jnp.einsum("bsd,dhe->bshe", normed, w_query, preferred_element_type=jnp.float32), cos_t, sin_t)
    k_loc = apply_rope(jnp.einsum("bsd,dhe->bshe", normed, w_key, preferred_element_type=jnp.float32), cos_t, sin_t)
    v_loc = jnp.einsum("bsd,dhe->bshe", normed, w_value, preferred_element_type=jnp.float32).astype(jnp.bfloat16)
    q_all = lax.all_to_all(q_loc, "seq", 2, 1, tiled=True)
    k_all = lax.all_to_all(k_loc, "seq", 2, 1, tiled=True)
    v_all = lax.all_to_all(v_loc, "seq", 2, 1, tiled=True)
    n_batch, seq_len, heads_loc, head_dim = q_all.shape
    kv_loc = k_all.shape[2]
    q_grouped = q_all.reshape(n_batch, seq_len, kv_loc, heads_loc // kv_loc, head_dim)
    attn_heads = causal_attention(q_grouped, k_all, v_all, 0, min(256, seq_len))
    attn_loc = lax.all_to_all(attn_heads, "seq", 1, 2, tiled=True)
    resid_h = (hidden.astype(jnp.float32) + jnp.einsum("bshe,hed->bsd", attn_loc, w_out, preferred_element_type=jnp.float32)).astype(jnp.bfloat16)
    normed_mlp = rms_norm(resid_h, gain_mlp)
    gelu_act = jax.nn.gelu(jnp.einsum("bsd,df->bsf", normed_mlp, w_up, preferred_element_type=jnp.float32), approximate=True).astype(jnp.bfloat16)
    layer_out = resid_h.astype(jnp.float32) + jnp.einsum("bsf,fd->bsd", gelu_act, w_down, preferred_element_type=jnp.float32)
    return layer_out.astype(jnp.bfloat16)


def solution(mesh):
    tok_spec = P(None, ("data", "seq"), None)
    in_specs = (tok_spec, P(("data", "seq"))) + (P(),) * 8

    def device_fn(x_loc, pos_loc, w_query, w_key, w_value, w_out, w_up, w_down, g_attn, g_mlp):
        cos_t, sin_t = rope_tables(pos_loc, w_query.shape[-1])
        hidden = x_loc
        for layer_idx in range(w_query.shape[0]):
            hidden = layer_step(hidden, cos_t, sin_t, w_query[layer_idx], w_key[layer_idx], w_value[layer_idx], w_out[layer_idx], w_up[layer_idx], w_down[layer_idx], g_attn[layer_idx], g_mlp[layer_idx])
        return hidden

    return jax.shard_map(device_fn, mesh=mesh, in_specs=in_specs, out_specs=tok_spec, check_vma=False)
```

profile of v0, /device:TPU:112, one launch (start us, length us, event | category | flops | bytes accessed | tf_op | source)
XLA Modules:
  0.0 3003.4 jit_solution(16316361878223572255)
XLA Ops:
  88.4 26.7 fusion.158
  199.2 85.0 %all-to-all-done.1 = bf16[12,128,24,128]{1,3,0,2:T(8,128)(2,1)} async-done(((bf16[12,128,24,128]{1,3,0,2:T(8,128)(2,1)}), bf16[12,128,24,128]{1,3,0,2:T(8,128)(2,1)}, u32[]{:S(2)}, u32[]{:S(2)}) %all-to-all-start.1) | async-done | bytes 9437216 | tf_op jit(solution)/shard_map/all_to_all | solution.py:60
  345.2 49.8 %all-to-all-done = bf16[12,128,24,128]{1,3,0,2:T(8,128)(2,1)} async-done(((bf16[12,128,24,128]{1,3,0,2:T(8,128)(2,1)}), bf16[12,128,24,128]{1,3,0,2:T(8,128)(2,1)}, u32[]{:S(2)}, u32[]{:S(2)}) %all-to-all-start) | async-done | bytes 9437216 | tf_op jit(solution)/shard_map/all_to_all | solution.py:59
  425.7 80.3 %all-to-all-done.2 = bf16[12,128,24,128]{3,1,0,2:T(8,128)(2,1)} async-done(((bf16[12,128,24,128]{3,1,0,2:T(8,128)(2,1)}), bf16[12,128,24,128]{3,1,0,2:T(8,128)(2,1)}, u32[]{:S(2)}, u32[]{:S(2)}) %all-to-all-start.2) | async-done | bytes 9437216 | tf_op jit(solution)/shard_map/all_to_all | solution.py:61
  523.4 218.8 %while.33 = (s32[]{:T(128)}, bf16[4,12,256,3,1,128]{5,2,0,3,1,4:T(8,128)(2,1)}, s32[4]{0:T(128)S(1)}, bf16[12,1024,3,1,128]{4,1,2,0,3:T(8,128)(2,1)}, bf16[12,10...) while((s32[]{:T(128)}, ...), condition=%wide.region_4.5_spmd.clone, body=%wide.region_1.4_spmd.clone.sunk | while | flops 4938250240 | bytes 166386432 | solution.py:50
  796.4 105.6 %all-to-all-done.3 = bf16[12,1024,3,128]{3,2,0,1:T(4,128)(2,1)} async-done(((bf16[12,1024,3,128]{3,2,0,1:T(4,128)(2,1)}), bf16[12,1024,3,128]{3,2,0,1:T(4,128)(2,1)}, u32[]{:S(2)}, u32[]{:S(2)}) %all-to-all-start.3) | async-done | bytes 9437216 | tf_op jit(solution)/shard_map/all_to_all | solution.py:66
  952.7 70.2 %fusion.183.clone.5 = bf16[12,128,8192]{2,1,0:T(8,128)(2,1)} fusion(bf16[3,2048,8192]{2,1,0:T(8,128)(2,1)} %param.22, bf16[12,128,2048]{2,1,0:T(8,128)(2,1)S(1)} %get-tuple-element.239, f32[2048]{0:T(1024)S(1)} %bitcast.486, f32[12,128]{1,0:T(8,128)S(1)} %add_rsqrt_fusion.4), kind=kOutput, calls=%fused_computation.79.clone.clone.clone.clone.clone.clone.2 | convolution fusion | flops 51665436672 | bytes 65026048 | tf_op jit(solution)/shard_map/bsd,df->bsf/dot_general | solution.py:69
  1022.9 68.5 %fusion.125 = (f32[12,128]{1,0:T(8,128)S(1)}, bf16[12,128,2048]{2,1,0:T(8,128)(2,1)}) fusion(bf16[3,8192,2048]{2,1,0:T(8,128)(2,1)} %param.23, bf16[12,128,2048]{2,1,0:T(8,128)(2,1)} %copy-done.14, bf16[12,128,8192]{2,1,0:T(8,128)(2,1)} %fusion.183.clone.5), kind=kOutput, calls=%fused_computation.149 | convolution fusion | flops 51558481920 | bytes 71309312 | tf_op jit(solution)/shard_map/bsf,fd->bsd/dot_general | solution.py:70
  1091.4 27.0 fusion.166
  1162.2 26.6 fusion.152
  1267.4 84.9 %all-to-all-done.5 = bf16[12,128,24,128]{1,3,0,2:T(8,128)(2,1)} async-done(((bf16[12,128,24,128]{1,3,0,2:T(8,128)(2,1)}), bf16[12,128,24,128]{1,3,0,2:T(8,128)(2,1)}, u32[]{:S(2)}, u32[]{:S(2)}) %all-to-all-start.5) | async-done | bytes 9437216 | tf_op jit(solution)/shard_map/all_to_all | solution.py:60
  1381.9 81.3 %all-to-all-done.4 = bf16[12,128,24,128]{1,3,0,2:T(8,128)(2,1)} async-done(((bf16[12,128,24,128]{1,3,0,2:T(8,128)(2,1)}), bf16[12,128,24,128]{1,3,0,2:T(8,128)(2,1)}, u32[]{:S(2)}, u32[]{:S(2)}) %all-to-all-start.4) | async-done | bytes 9437216 | tf_op jit(solution)/shard_map/all_to_all | solution.py:59
  1481.8 219.2 %while.34 = (s32[]{:T(128)}, bf16[4,12,256,3,1,128]{5,2,0,3,1,4:T(8,128)(2,1)}, s32[4]{0:T(128)S(1)}, bf16[12,1024,3,1,128]{4,1,2,0,3:T(8,128)(2,1)}, bf16[12,10...) while((s32[]{:T(128)}, ...), condition=%wide.region_10.11_spmd.clone, body=%wide.region_7.10_spmd.clone.sunk | while | flops 4938250240 | bytes 166386432 | solution.py:50
  1754.6 106.2 %all-to-all-done.7 = bf16[12,1024,3,128]{3,2,0,1:T(4,128)(2,1)} async-done(((bf16[12,1024,3,128]{3,2,0,1:T(4,128)(2,1)}), bf16[12,1024,3,128]{3,2,0,1:T(4,128)(2,1)}, u32[]{:S(2)}, u32[]{:S(2)}) %all-to-all-start.7) | async-done | bytes 9437216 | tf_op jit(solution)/shard_map/all_to_all | solution.py:66
  1911.5 70.7 %fusion.195.clone.5 = bf16[12,128,8192]{2,1,0:T(8,128)(2,1)} fusion(bf16[3,2048,8192]{2,1,0:T(8,128)(2,1)} %param.22, bf16[12,128,2048]{2,1,0:T(8,128)(2,1)S(1)} %get-tuple-element.243, f32[2048]{0:T(1024)S(1)} %bitcast.482, f32[12,128]{1,0:T(8,128)S(1)} %add_rsqrt_fusion.2), kind=kOutput, calls=%fused_computation.87.clone.clone.clone.clone.clone.clone.2 | convolution fusion | flops 51665436672 | bytes 65026048 | tf_op jit(solution)/shard_map/bsd,df->bsf/dot_general | solution.py:69
  1982.2 68.5 %fusion.133 = (f32[12,128]{1,0:T(8,128)S(1)}, bf16[12,128,2048]{2,1,0:T(8,128)(2,1)}) fusion(bf16[3,8192,2048]{2,1,0:T(8,128)(2,1)} %param.23, bf16[12,128,2048]{2,1,0:T(8,128)(2,1)} %copy-done.13, bf16[12,128,8192]{2,1,0:T(8,128)(2,1)} %fusion.195.clone.5), kind=kOutput, calls=%fused_computation.157 | convolution fusion | flops 51558481920 | bytes 71309312 | tf_op jit(solution)/shard_map/bsf,fd->bsd/dot_general | solution.py:70
  2050.7 27.0 fusion.167
  2121.5 26.6 fusion.146
  2226.7 84.9 %all-to-all-done.9 = bf16[12,128,24,128]{1,3,0,2:T(8,128)(2,1)} async-done(((bf16[12,128,24,128]{1,3,0,2:T(8,128)(2,1)}), bf16[12,128,24,128]{1,3,0,2:T(8,128)(2,1)}, u32[]{:S(2)}, u32[]{:S(2)}) %all-to-all-start.9) | async-done | bytes 9437216 | tf_op jit(solution)/shard_map/all_to_all | solution.py:60
  2341.1 81.3 %all-to-all-done.8 = bf16[12,128,24,128]{1,3,0,2:T(8,128)(2,1)} async-done(((bf16[12,128,24,128]{1,3,0,2:T(8,128)(2,1)}), bf16[12,128,24,128]{1,3,0,2:T(8,128)(2,1)}, u32[]{:S(2)}, u32[]{:S(2)}) %all-to-all-start.8) | async-done | bytes 9437216 | tf_op jit(solution)/shard_map/all_to_all | solution.py:59
  2441.1 218.9 %while.35 = (s32[]{:T(128)}, bf16[4,12,256,3,1,128]{5,2,0,3,1,4:T(8,128)(2,1)}, s32[4]{0:T(128)S(1)}, bf16[12,1024,3,1,128]{4,1,2,0,3:T(8,128)(2,1)}, bf16[12,10...) while((s32[]{:T(128)}, ...), condition=%wide.region_16.17_spmd.clone, body=%wide.region_13.16_spmd.clone.sunk | while | flops 4938250240 | bytes 166386432 | solution.py:50
  2673.9 143.3 %all_to_all.207 = bf16[12,1024,3,128]{3,2,0,1:T(4,128)(2,1)} all-to-all(bf16[12,1024,3,128]{3,2,0,1:T(4,128)(2,1)S(1)} %copy.89), channel_id=1, replica_groups=mesh['data'=2,'seq'=8] {'seq'}, dimensions={1} | all-to-all | bytes 18874368 | tf_op jit(solution)/shard_map/all_to_all | solution.py:66
  2865.1 70.5 %fusion.297 = bf16[12,128,8192]{2,1,0:T(8,128)(2,1)} fusion(bf16[3,2048,8192]{2,1,0:T(8,128)(2,1)} %param.22, bf16[12,128,2048]{2,1,0:T(8,128)(2,1)S(1)} %get-tuple-element.247, f32[2048]{0:T(1024)S(1)} %bitcast.478, f32[12,128]{1,0:T(8,128)S(1)} %add_rsqrt_fusion), kind=kOutput, calls=%fused_computation.95.clone.clone.clone.clone.2 | convolution fusion | flops 51665436672 | bytes 65026048 | tf_op jit(solution)/shard_map/bsd,df->bsf/dot_general | solution.py:69
  2935.6 67.6 %fusion.140 = bf16[12,128,2048]{2,1,0:T(8,128)(2,1)} fusion(bf16[12,128,2048]{2,1,0:T(8,128)(2,1)S(1)} %get-tuple-element.247, bf16[3,8192,2048]{2,1,0:T(8,128)(2,1)} %param.23, bf16[12,128,8192]{2,1,0:T(8,128)(2,1)} %fusion.297), kind=kOutput, calls=%fused_computation.164 | convolution fusion | flops 51549044736 | bytes 71303168 | tf_op jit(solution)/shard_map/bsf,fd->bsd/dot_general | solution.py:70
  (274 shorter events, 1541.8 us)
Async XLA Ops:
  71.8 43.4 %slice-start.9 = ((s8[6291456]{0:T(1024)(128)(4,1)}), s8[2097152]{0:T(1024)(128)(4,1)S(1)}, s32[]{:S(2)}) async-start(s8[6291456]{0:T(1024)(128)(4,1)} %bitcast.470), calls=%async_computation.21 | async-start | bytes 4194304
  172.4 111.7 %all-to-all-start.1 = ((bf16[12,128,24,128]{1,3,0,2:T(8,128)(2,1)}), bf16[12,128,24,128]{1,3,0,2:T(8,128)(2,1)}, u32[]{:S(2)}, u32[]{:S(2)}) async-start(bf16[12,128,24,128]{1,3,0,2:T(8,128)(2,1)} %copy.57), calls=%async_computation.1 | async-start | bytes 18874368 | tf_op jit(solution)/shard_map/all_to_all | solution.py:60
  284.1 110.8 %all-to-all-start = ((bf16[12,128,24,128]{1,3,0,2:T(8,128)(2,1)}), bf16[12,128,24,128]{1,3,0,2:T(8,128)(2,1)}, u32[]{:S(2)}, u32[]{:S(2)}) async-start(bf16[12,128,24,128]{1,3,0,2:T(8,128)(2,1)} %copy.54), calls=%async_computation | async-start | bytes 18874368 | tf_op jit(solution)/shard_map/all_to_all | solution.py:59
  395.0 111.0 %all-to-all-start.2 = ((bf16[12,128,24,128]{3,1,0,2:T(8,128)(2,1)}), bf16[12,128,24,128]{3,1,0,2:T(8,128)(2,1)}, u32[]{:S(2)}, u32[]{:S(2)}) async-start(bf16[12,128,24,128]{3,1,0,2:T(8,128)(2,1)} %copy.60), calls=%async_computation.2 | async-start | bytes 18874368 | tf_op jit(solution)/shard_map/all_to_all | solution.py:61
  524.9 35.3 %slice-start.6 = ((s8[9437184]{0:T(1024)(128)(4,1)}), s8[4194304]{0:T(1024)(128)(4,1)S(1)}, s32[]{:S(2)}) async-start(s8[9437184]{0:T(1024)(128)(4,1)} %bitcast.465), calls=%async_computation.18 | async-start | bytes 8388608 | tf_op jit(solution)/shard_map/while
  579.6 35.3 %slice-start.6 = ((s8[9437184]{0:T(1024)(128)(4,1)}), s8[4194304]{0:T(1024)(128)(4,1)S(1)}, s32[]{:S(2)}) async-start(s8[9437184]{0:T(1024)(128)(4,1)} %bitcast.465), calls=%async_computation.18 | async-start | bytes 8388608 | tf_op jit(solution)/shard_map/while
  689.0 35.3 %slice-start.6 = ((s8[9437184]{0:T(1024)(128)(4,1)}), s8[4194304]{0:T(1024)(128)(4,1)S(1)}, s32[]{:S(2)}) async-start(s8[9437184]{0:T(1024)(128)(4,1)} %bitcast.465), calls=%async_computation.18 | async-start | bytes 8388608 | tf_op jit(solution)/shard_map/while
  757.1 144.9 %all-to-all-start.3 = ((bf16[12,1024,3,128]{3,2,0,1:T(4,128)(2,1)}), bf16[12,1024,3,128]{3,2,0,1:T(4,128)(2,1)}, u32[]{:S(2)}, u32[]{:S(2)}) async-start(bf16[12,1024,3,128]{3,2,0,1:T(4,128)(2,1)} %copy.63), calls=%async_computation.3 | async-start | bytes 25165824 | tf_op jit(solution)/shard_map/all_to_all | solution.py:66
  1022.9 68.5 %copy-start.10 = (f32[1,2048]{1,0:T(1,128)S(1)}, f32[1,2048]{1,0:T(1,128)}, u32[]{:S(2)}) copy-start(f32[1,2048]{1,0:T(1,128)} %get-tuple-element.235) | copy-start | bytes 24580
  1130.0 111.3 %all-to-all-start.6 = ((bf16[12,128,24,128]{3,1,0,2:T(8,128)(2,1)}), bf16[12,128,24,128]{3,1,0,2:T(8,128)(2,1)}, u32[]{:S(2)}, u32[]{:S(2)}) async-start(bf16[12,128,24,128]{3,1,0,2:T(8,128)(2,1)} %copy.73), calls=%async_computation.6 | async-start | bytes 18874368 | tf_op jit(solution)/shard_map/all_to_all | solution.py:61
  1241.3 111.0 %all-to-all-start.5 = ((bf16[12,128,24,128]{1,3,0,2:T(8,128)(2,1)}), bf16[12,128,24,128]{1,3,0,2:T(8,128)(2,1)}, u32[]{:S(2)}, u32[]{:S(2)}) async-start(bf16[12,128,24,128]{1,3,0,2:T(8,128)(2,1)} %copy.70), calls=%async_computation.5 | async-start | bytes 18874368 | tf_op jit(solution)/shard_map/all_to_all | solution.py:60
  1352.3 110.8 %all-to-all-start.4 = ((bf16[12,128,24,128]{1,3,0,2:T(8,128)(2,1)}), bf16[12,128,24,128]{1,3,0,2:T(8,128)(2,1)}, u32[]{:S(2)}, u32[]{:S(2)}) async-start(bf16[12,128,24,128]{1,3,0,2:T(8,128)(2,1)} %copy.67), calls=%async_computation.4 | async-start | bytes 18874368 | tf_op jit(solution)/shard_map/all_to_all | solution.py:59
  1483.4 35.3 %slice-start.3 = ((s8[9437184]{0:T(1024)(128)(4,1)}), s8[4194304]{0:T(1024)(128)(4,1)S(1)}, s32[]{:S(2)}) async-start(s8[9437184]{0:T(1024)(128)(4,1)} %bitcast.462), calls=%async_computation.15 | async-start | bytes 8388608 | tf_op jit(solution)/shard_map/while
  1538.2 35.3 %slice-start.3 = ((s8[9437184]{0:T(1024)(128)(4,1)}), s8[4194304]{0:T(1024)(128)(4,1)S(1)}, s32[]{:S(2)}) async-start(s8[9437184]{0:T(1024)(128)(4,1)} %bitcast.462), calls=%async_computation.15 | async-start | bytes 8388608 | tf_op jit(solution)/shard_map/while
  1593.0 35.3 %slice-start.3 = ((s8[9437184]{0:T(1024)(128)(4,1)}), s8[4194304]{0:T(1024)(128)(4,1)S(1)}, s32[]{:S(2)}) async-start(s8[9437184]{0:T(1024)(128)(4,1)} %bitcast.462), calls=%async_computation.15 | async-start | bytes 8388608 | tf_op jit(solution)/shard_map/while
  1647.8 35.3 %slice-start.3 = ((s8[9437184]{0:T(1024)(128)(4,1)}), s8[4194304]{0:T(1024)(128)(4,1)S(1)}, s32[]{:S(2)}) async-start(s8[9437184]{0:T(1024)(128)(4,1)} %bitcast.462), calls=%async_computation.15 | async-start | bytes 8388608 | tf_op jit(solution)/shard_map/while
  1716.0 144.9 %all-to-all-start.7 = ((bf16[12,1024,3,128]{3,2,0,1:T(4,128)(2,1)}), bf16[12,1024,3,128]{3,2,0,1:T(4,128)(2,1)}, u32[]{:S(2)}, u32[]{:S(2)}) async-start(bf16[12,1024,3,128]{3,2,0,1:T(4,128)(2,1)} %copy.76), calls=%async_computation.7 | async-start | bytes 25165824 | tf_op jit(solution)/shard_map/all_to_all | solution.py:66
  1982.2 68.5 %copy-start.8 = (f32[1,2048]{1,0:T(1,128)S(1)}, f32[1,2048]{1,0:T(1,128)}, u32[]{:S(2)}) copy-start(f32[1,2048]{1,0:T(1,128)} %get-tuple-element.233) | copy-start | bytes 24580
  2089.3 111.3 %all-to-all-start.10 = ((bf16[12,128,24,128]{3,1,0,2:T(8,128)(2,1)}), bf16[12,128,24,128]{3,1,0,2:T(8,128)(2,1)}, u32[]{:S(2)}, u32[]{:S(2)}) async-start(bf16[12,128,24,128]{3,1,0,2:T(8,128)(2,1)} %copy.86), calls=%async_computation.10 | async-start | bytes 18874368 | tf_op jit(solution)/shard_map/all_to_all | solution.py:61
  2200.6 111.0 %all-to-all-start.9 = ((bf16[12,128,24,128]{1,3,0,2:T(8,128)(2,1)}), bf16[12,128,24,128]{1,3,0,2:T(8,128)(2,1)}, u32[]{:S(2)}, u32[]{:S(2)}) async-start(bf16[12,128,24,128]{1,3,0,2:T(8,128)(2,1)} %copy.83), calls=%async_computation.9 | async-start | bytes 18874368 | tf_op jit(solution)/shard_map/all_to_all | solution.py:60
  2311.6 110.8 %all-to-all-start.8 = ((bf16[12,128,24,128]{1,3,0,2:T(8,128)(2,1)}), bf16[12,128,24,128]{1,3,0,2:T(8,128)(2,1)}, u32[]{:S(2)}, u32[]{:S(2)}) async-start(bf16[12,128,24,128]{1,3,0,2:T(8,128)(2,1)} %copy.80), calls=%async_computation.8 | async-start | bytes 18874368 | tf_op jit(solution)/shard_map/all_to_all | solution.py:59
  2442.6 35.3 %slice-start = ((s8[9437184]{0:T(1024)(128)(4,1)}), s8[4194304]{0:T(1024)(128)(4,1)S(1)}, s32[]{:S(2)}) async-start(s8[9437184]{0:T(1024)(128)(4,1)} %bitcast.459), calls=%async_computation.12 | async-start | bytes 8388608 | tf_op jit(solution)/shard_map/while
  2552.0 35.3 %slice-start = ((s8[9437184]{0:T(1024)(128)(4,1)}), s8[4194304]{0:T(1024)(128)(4,1)S(1)}, s32[]{:S(2)}) async-start(s8[9437184]{0:T(1024)(128)(4,1)} %bitcast.459), calls=%async_computation.12 | async-start | bytes 8388608 | tf_op jit(solution)/shard_map/while
  2606.8 35.3 %slice-start = ((s8[9437184]{0:T(1024)(128)(4,1)}), s8[4194304]{0:T(1024)(128)(4,1)S(1)}, s32[]{:S(2)}) async-start(s8[9437184]{0:T(1024)(128)(4,1)} %bitcast.459), calls=%async_computation.12 | async-start | bytes 8388608 | tf_op jit(solution)/shard_map/while
  (40 other events, 996.9 us)
where the time goes:
time: 3020 us; the launch traced here: 3000 us
  matrix products  1160 us (38%)
  waiting for transfers between devices  797 us (26%)
  local copies, waits for them, and re-layouts  529 us (18%)
  other arithmetic  307 us (10%)
  blocking collectives  143 us (5%)
  starting transfers between devices  60.2 us (2%)
    all_to_all x3, waiting for transfers between devices, layer_step(): k_all = lax.all_to_all(k_loc, 'seq', 2, 1, tiled=True)  255 us
    dot_general x12, matrix products, one_block(): jnp.einsum('bqkgd,bskd->bkgqs', q_blk, k_heads, preferred_element_type=jn...  216 us
    dot_general x12, matrix products, one_block(): jnp.einsum('bkgqs,bskd->bqkgd', exp_f32.astype(jnp.bfloat16), v_heads, pr...  215 us
    all_to_all x3, waiting for transfers between devices, layer_step(): q_all = lax.all_to_all(q_loc, 'seq', 2, 1, tiled=True)  212 us
    all_to_all x2, waiting for transfers between devices, layer_step(): attn_loc = lax.all_to_all(attn_heads, 'seq', 1, 2, tiled=True)  212 us
    dot_general x3, matrix products, layer_step(): jnp.einsum('bsd,df->bsf', normed_mlp, w_up, preferred_element_type=jnp.fl...  211 us
    reduce_sum x12, other arithmetic, one_block(): row_sum = jnp.sum(exp_f32, axis=-1)  207 us
    dot_general x3, matrix products, layer_step(): jnp.einsum('bsf,fd->bsd', gelu_act, w_down, preferred_element_type=jnp.fl...  205 us
  transfers between devices with their start and end apart: 11, of which 11 were waited for; matrix products, arithmetic and copies ran while one was open for 14% of the time, Pallas kernels for 0%

commit v1 on v0

v1 whole, which is shorter than its diff:
```python
import functools

import jax
import jax.numpy as jnp
from jax import lax
from jax.experimental import pallas as pl
from jax.experimental.pallas import tpu as pltpu
from jax.sharding import PartitionSpec as P

ROPE_BASE = 10000.0
NORM_EPS = 1e-6
MASKED = -1e30
VMEM_LIMIT = 62 * 2**20


def norm_rows(x_f32, gain_row):
    mean_sq = jnp.mean(x_f32 * x_f32, axis=-1, keepdims=True)
    return (x_f32 * lax.rsqrt(mean_sq + NORM_EPS) * gain_row).astype(jnp.bfloat16)


def qkv_kernel(steps, sub, x_ref, wq_ref, wk_ref, wv_ref, cos_ref, sin_ref, out_ref):
    step = pl.program_id(0)
    rows = x_ref.shape[0]
    depth, hb, dh = wq_ref.shape

    def project(w_ref, rotate):
        w = w_ref[...].reshape(depth, hb * dh)
        for r in range(0, rows, sub):
            acc = jnp.dot(x_ref[r : r + sub, :], w, preferred_element_type=jnp.float32)
            if rotate:
                cos, sin = cos_ref[r : r + sub, :], sin_ref[r : r + sub, :]
                for h in range(hb):
                    u = acc[:, h * dh : (h + 1) * dh]
                    rot = u * cos + pltpu.roll(u, dh // 2, 1) * sin
                    out_ref[r : r + sub, h * dh : (h + 1) * dh] = rot.astype(jnp.bfloat16)
            else:
                out_ref[r : r + sub, :] = acc.astype(jnp.bfloat16)

    pl.when(step < steps)(lambda: project(wq_ref, True))
    pl.when((step >= steps) & (step < 2 * steps))(lambda: project(wk_ref, True))
    pl.when(step >= 2 * steps)(lambda: project(wv_ref, False))


def qkv_project(x, w_query, w_key, w_value, cos, sin, layer):
    rows, depth = x.shape
    heads, dh = w_query.shape[2:]
    hb = 8
    steps = heads // hb
    w_spec = lambda part: pl.BlockSpec(
        (None, depth, hb, dh), lambda i: (layer, 0, jnp.clip(i - part * steps, 0, steps - 1), 0)
    )
    const = lambda shape: pl.BlockSpec(shape, lambda i: (0, 0))
    return pl.pallas_call(
        functools.partial(qkv_kernel, steps, 512),
        grid=(3 * steps,),
        in_specs=[const((rows, depth)), w_spec(0), w_spec(1), w_spec(2), const((rows, dh)), const((rows, dh))],
        out_specs=pl.BlockSpec((rows, hb * dh), lambda i: (0, i)),
        out_shape=jax.ShapeDtypeStruct((rows, 3 * heads * dh), jnp.bfloat16),
        compiler_params=pltpu.CompilerParams(vmem_limit_bytes=VMEM_LIMIT),
        cost_estimate=pl.CostEstimate(
            flops=6 * rows * depth * heads * dh, bytes_accessed=6 * depth * heads * dh, transcendentals=0
        ),
        name="qkv_project",
    )(x, w_query, w_key, w_value, cos, sin)


def scores(q, k):
    return lax.dot_general(q, k, (((1,), (1,)), ((), ())), preferred_element_type=jnp.float32)


def softmax_sum(score_list, value_list, scale2):
    row_max = functools.reduce(jnp.maximum, [jnp.max(s, axis=-1, keepdims=True) for s in score_list])
    offset = row_max * scale2
    exps = [jnp.exp2(s * scale2 - offset) for s in score_list]
    row_sum = sum(jnp.sum(e, axis=-1, keepdims=True) for e in exps)
    out = sum(
        jnp.dot(e.astype(jnp.bfloat16), v, preferred_element_type=jnp.float32) for e, v in zip(exps, value_list)
    )
    return (out * (1.0 / row_sum)).astype(jnp.bfloat16)


def whole_kernel(tile, scale2, dh, q_ref, k_ref, v_ref, out_ref):
    n_tok, width = q_ref.shape
    causal = lax.broadcasted_iota(jnp.int32, (tile, tile), 1) <= lax.broadcasted_iota(jnp.int32, (tile, tile), 0)
    for c0 in range(0, width, dh):
        cols = slice(c0, c0 + dh)
        for t in range(0, n_tok, tile):
            here = slice(t, t + tile)
            q = q_ref[here, cols]
            parts = [jnp.where(causal, scores(q, k_ref[here, cols]), MASKED)]
            values = [v_ref[here, cols]]
            if t:
                parts.append(scores(q, k_ref[:t, cols]))
                values.append(v_ref[:t, cols])
            out_ref[here, cols] = softmax_sum(parts, values, scale2)


def half_kernel(tile, piece, scale2, dh, core_ref, q_ref, k_ref, v_ref, k2_ref, v2_ref, prev_ref, out_ref):
    n_tok, width = q_ref.shape
    core = core_ref[0]
    key = lax.broadcasted_iota(jnp.int32, (tile, tile), 1)
    query = lax.broadcasted_iota(jnp.int32, (tile, tile), 0)
    causal = key <= query
    causal2 = key // piece < query // piece + core
    for c0 in range(0, width, dh):
        cols = slice(c0, c0 + dh)
        for t in range(0, n_tok, tile):
            here = slice(t, t + tile)
            q = q_ref[here, cols]
            parts = [
                jnp.where(causal, scores(q, k_ref[here, cols]), MASKED),
                jnp.where(causal2, scores(q, k2_ref[here, cols]), MASKED),
            ]
            values = [v_ref[here, cols], v2_ref[here, cols]]
            if t:
                parts += [scores(q, k_ref[:t, cols]), scores(q, k2_ref[:t, cols])]
                values += [v_ref[:t, cols], v2_ref[:t, cols]]
            out_ref[here, cols] = softmax_sum(parts, values, scale2)


def attention(qkv, kv_other, core, n_whole, piece, heads, dh):
    rows = qkv.shape[0]
    n_half = rows - n_whole
    tile = 256
    scale2 = float(dh**-0.5 * 1.4426950408889634)
    group = 2
    width = group * dh
    steps = heads // group
    params = pltpu.CompilerParams(vmem_limit_bytes=VMEM_LIMIT)
    out_shape = jax.ShapeDtypeStruct((rows, heads * dh), jnp.bfloat16)
    whole = lambda part: pl.BlockSpec((n_whole, width), lambda h: (0, part * steps + h))
    out = pl.pallas_call(
        functools.partial(whole_kernel, tile, scale2, dh),
        grid=(steps,),
        in_specs=[whole(0), whole(1), whole(2)],
        out_specs=whole(0),
        out_shape=out_shape,
        compiler_params=params,
        cost_estimate=pl.CostEstimate(
            flops=8 * n_whole * n_whole * heads * dh, bytes_accessed=8 * n_whole * heads * dh, transcendentals=0
        ),
        name="attend_whole",
    )(qkv, qkv, qkv)
    skip = n_whole // n_half
    half = lambda part: pl.BlockSpec((n_half, width), lambda h: (skip, part * steps + h))
    other = lambda part: pl.BlockSpec((n_half, width), lambda h: (0, part * steps + h))
    return pl.pallas_call(
        functools.partial(half_kernel, tile, piece, scale2, dh),
        grid=(steps,),
        in_specs=[
            pl.BlockSpec(memory_space=pltpu.SMEM),
            half(0),
            half(1),
            half(2),
            other(0),
            other(1),
            pl.BlockSpec(memory_space=pl.ANY),
        ],
        out_specs=half(0),
        out_shape=out_shape,
        input_output_aliases={6: 0},
        compiler_params=params,
        cost_estimate=pl.CostEstimate(
            flops=8 * n_half * n_half * heads * dh, bytes_accessed=12 * n_half * heads * dh, transcendentals=0
        ),
        name="attend_half",
    )(core, qkv, qkv, qkv, kv_other, kv_other, out)


def out_kernel(sub, o_ref, x_ref, w_ref, g_ref, h_ref, r_ref):
    for r in range(0, o_ref.shape[0], sub):
        prod = jnp.dot(o_ref[r : r + sub, :], w_ref[...], preferred_element_type=jnp.float32)
        h = (x_ref[r : r + sub, :].astype(jnp.float32) + prod).astype(jnp.bfloat16)
        h_ref[r : r + sub, :] = h
        r_ref[r : r + sub, :] = norm_rows(h.astype(jnp.float32), g_ref[...])


def out_project(o, x, w_out, gain, layer):
    rows, depth = o.shape
    width = x.shape[1]
    mb = 512
    row_spec = lambda n: pl.BlockSpec((mb, n), lambda m: (m, 0))
    return pl.pallas_call(
        functools.partial(out_kernel, 256),
        grid=(rows // mb,),
        in_specs=[
            row_spec(depth),
            row_spec(width),
            pl.BlockSpec((None, depth, width), lambda m: (layer, 0, 0), pipeline_mode=pl.Buffered(1)),
            pl.BlockSpec((1, width), lambda m: (0, 0)),
        ],
        out_specs=[row_spec(width)] * 2,
        out_shape=[jax.ShapeDtypeStruct((rows, width), jnp.bfloat16)] * 2,
        compiler_params=pltpu.CompilerParams(vmem_limit_bytes=VMEM_LIMIT),
        cost_estimate=pl.CostEstimate(
            flops=2 * rows * depth * width, bytes_accessed=2 * depth * width, transcendentals=0
        ),
        name="out_project",
    )(o, x, w_out, gain)


def mlp_kernel(sub, r_ref, h_ref, up_ref, down_ref, g_ref, y_ref, n_ref, acc):
    f = pl.program_id(1)
    rows = r_ref.shape[0]

    @pl.when(f == 0)
    def _():
        acc[...] = jnp.zeros_like(acc)

    for r in range(0, rows, sub):
        u = jnp.dot(r_ref[r : r + sub, :], up_ref[...], preferred_element_type=jnp.float32)
        z = jax.nn.gelu(u, approximate=True).astype(jnp.bfloat16)
        acc[r : r + sub, :] += jnp.dot(z, down_ref[...], preferred_element_type=jnp.float32)

    @pl.when(f == pl.num_programs(1) - 1)
    def _():
        for r in range(0, rows, 256):
            y = (h_ref[r : r + 256, :].astype(jnp.float32) + acc[r : r + 256, :]).astype(jnp.bfloat16)
            y_ref[r : r + 256, :] = y
            n_ref[r : r + 256, :] = norm_rows(y.astype(jnp.float32), g_ref[...])


def mlp(r, h, w_up, w_down, gain, layer):
    rows, width = r.shape
    ff = w_up.shape[2]
    mb, tf, sub = 768, 1024, 384
    row_spec = pl.BlockSpec((mb, width), lambda m, f: (m, 0))
    return pl.pallas_call(
        functools.partial(mlp_kernel, sub),
        grid=(rows // mb, ff // tf),
        in_specs=[
            row_spec,
            row_spec,
            pl.BlockSpec((None, width, tf), lambda m, f: (layer, 0, f)),
            pl.BlockSpec((None, tf, width), lambda m, f: (layer, f, 0)),
            pl.BlockSpec((1, width), lambda m, f: (0, 0)),
        ],
        out_specs=[row_spec] * 2,
        out_shape=[jax.ShapeDtypeStruct((rows, width), jnp.bfloat16)] * 2,
        scratch_shapes=[pltpu.VMEM((mb, width), jnp.float32)],
        compiler_params=pltpu.CompilerParams(vmem_limit_bytes=VMEM_LIMIT),
        cost_estimate=pl.CostEstimate(
            flops=4 * rows * ff * width, bytes_accessed=4 * ff * width, transcendentals=0
        ),
        name="mlp",
    )(r, h, w_up, w_down, gain)


def solution(mesh):
    n_seq = mesh.shape["seq"]
    n_pair = n_seq // 2
    tok_spec = P(None, ("data", "seq"), None)
    in_specs = (tok_spec, P(("data", "seq"))) + (P(),) * 8
    partner = [(i, i ^ 1) for i in range(n_seq)]

    def device_fn(x_loc, pos_loc, w_query, w_key, w_value, w_out, w_up, w_down, g_attn, g_mlp):
        n_layers, _, heads, dh = w_query.shape
        n_batch, shard, width = x_loc.shape
        per = n_batch // n_pair
        assert per * n_pair == n_batch and per == 3
        piece = shard // 2
        core = lax.rem(lax.axis_index("seq"), 2)
        exchange = lambda a: lax.all_to_all(a, "seq", 0, 0, tiled=True)

        by_chip = x_loc.reshape(n_pair, per, shard, width)
        whole = exchange(by_chip[:, :2].reshape(n_seq, shard, width))
        half = exchange(by_chip[:, 2].reshape(n_seq, piece, width))
        hidden = jnp.concatenate([whole.reshape(n_seq * shard, width), half.reshape(n_seq * piece, width)])
        n_whole = n_seq * shard

        pos = lax.all_gather(pos_loc, "seq", tiled=True)
        pos_half = lax.dynamic_index_in_dim(pos.reshape(n_seq, 2, piece), core, axis=1, keepdims=False).reshape(-1)
        inv_freq = ROPE_BASE ** (-jnp.arange(dh // 2, dtype=jnp.float32) * (2.0 / dh))
        angles = jnp.concatenate([pos, pos_half]).astype(jnp.float32)[:, None] * inv_freq
        cos, sin = jnp.cos(angles), jnp.sin(angles)
        cos = jnp.concatenate([cos, cos], axis=-1)
        sin = jnp.concatenate([-sin, sin], axis=-1)
        core_arr = core.astype(jnp.int32).reshape(1)
        w_out2 = w_out.reshape(n_layers, heads * dh, width)

        normed = norm_rows(hidden.astype(jnp.float32), g_attn[0])
        for layer in range(n_layers):
            qkv = qkv_project(normed, w_query, w_key, w_value, cos, sin, layer)
            kv_other = lax.ppermute(qkv[n_whole:, heads * dh :], "seq", partner)
            attn = attention(qkv, kv_other, core_arr, n_whole, piece, heads, dh)
            resid, r = out_project(attn, hidden, w_out2, g_mlp[layer][None], layer)
            following = g_attn[min(layer + 1, n_layers - 1)][None]
            hidden, normed = mlp(r, resid, w_up, w_down, following, layer)

        whole = exchange(hidden[:n_whole].reshape(n_seq, shard, width)).reshape(n_pair, 2, shard, width)
        half = exchange(hidden[n_whole:].reshape(n_seq, piece, width)).reshape(n_pair, 1, shard, width)
        return jnp.concatenate([whole, half], axis=1).reshape(n_batch, shard, width)

    return jax.shard_map(device_fn, mesh=mesh, in_specs=in_specs, out_specs=tok_spec, check_vma=False)
```

time: 3020 us -> 1140 us (0.38)
  matrix products: 1160 us -> 0 us
  Pallas kernels: 0 us -> 885 us
  waiting for transfers between devices: 797 us -> 44.6 us
  local copies, waits for them, and re-layouts: 529 us -> 36.7 us
  other arithmetic: 307 us -> 27.1 us
  starting transfers between devices: 60.2 us -> 14.5 us
    dot_general x42 -> x0, matrix products: 1160 us -> none  [the longest x12 216 us: one_block(): jnp.einsum('bqkgd,bskd->bkgqs', q_blk, k_heads, preferred_element_type=jn...]
    pallas_call x0 -> x15, Pallas kernels: none -> 885 us  [the longest x3 387 us: mlp(): pl.pallas_call(functools.partial(mlp_kernel, sub), grid=(rows // mb, ff /...]
    all_to_all x11 -> x3, waiting for transfers between devices: 797 us -> 44.6 us  [device_fn(): exchange = lambda a: lax.all_to_all(a, 'seq', 0, 0, tiled=True)]
    reduce_sum x13 -> x1, other arithmetic: 212 us -> 3.48 us  [norm_rows(): mean_sq = jnp.mean(x_f32 * x_f32, axis=-1, keepdims=True)]
    all_to_all x15 -> x0, local copies, waits for them, and re-layouts: 178 us -> none  [the longest x6 67.6 us: layer_step(): attn_loc = lax.all_to_all(attn_heads, 'seq', 1, 2, tiled=True)]
    unnamed x40 -> x10, local copies, waits for them, and re-layouts: 105 us -> 0.02 us
    all_to_all x1, blocking collectives: 143 us -> 53.3 us  [device_fn(): exchange = lambda a: lax.all_to_all(a, 'seq', 0, 0, tiled=True)]
    concatenate x6 -> x1, local copies, waits for them, and re-layouts: 69.4 us -> 0.08 us  [device_fn(): jnp.concatenate([pos, pos_half]).astype(jnp.float32)[:, None] * inv_freq]
  transfers between devices with their start and end apart: 11 -> 6, of which waited for: 11 -> 2; matrix products, arithmetic and copies ran while one was open for 14% -> 2% of each run, Pallas kernels for 0% -> 11%
where the time goes in v1:
time: 1140 us; the launch traced here: 1130 us
  Pallas kernels  885 us (78%)
  blocking collectives  117 us (10%)
  waiting for transfers between devices  44.6 us (4%)
  local copies, waits for them, and re-layouts  36.7 us (3%)
  other arithmetic  27.1 us (2%)
  starting transfers between devices  14.5 us (1%)
    pallas_call x3, Pallas kernels, mlp(): pl.pallas_call(functools.partial(mlp_kernel, sub), grid=(rows // mb, ff /...  387 us
    pallas_call x3, Pallas kernels, qkv_project(): pl.pallas_call(functools.partial(qkv_kernel, steps, 512), grid=(3 * steps...  213 us
    pallas_call x3, Pallas kernels, attention(): pl.pallas_call(functools.partial(whole_kernel, tile, scale2, dh), grid=(s...  125 us
    pallas_call x3, Pallas kernels, out_project(): pl.pallas_call(functools.partial(out_kernel, 256), grid=(rows // mb,), in...  89.3 us
    pallas_call x3, Pallas kernels, attention(): pl.pallas_call(functools.partial(half_kernel, tile, piece, scale2, dh), g...  71.2 us
    all_gather x1, blocking collectives, device_fn(): pos = lax.all_gather(pos_loc, 'seq', tiled=True)  64.2 us
    all_to_all x1, blocking collectives, device_fn(): exchange = lambda a: lax.all_to_all(a, 'seq', 0, 0, tiled=True)  53.3 us
    all_to_all x3, waiting for transfers between devices, device_fn(): exchange = lambda a: lax.all_to_all(a, 'seq', 0, 0, tiled=True)  44.6 us
  transfers between devices with their start and end apart: 6, of which 2 were waited for; matrix products, arithmetic and copies ran while one was open for 2% of the time, Pallas kernels for 11%

profile of v1, /device:TPU:112, one launch (start us, length us, event | category | flops | bytes accessed | tf_op | source)
XLA Modules:
  0.0 1126.3 jit_solution(11336707959663115021)
XLA Ops:
  13.3 22.4 %all-to-all-done.1 = bf16[8,64,2048]{2,1,0:T(8,128)(2,1)S(1)} async-done(((bf16[8,64,2048]{2,1,0:T(8,128)(2,1)}), bf16[8,64,2048]{2,1,0:T(8,128)(2,1)S(1)}, u32[]{:S(2)}, u32[]{:S(2)}) %all-to-all-start.1) | async-done | bytes 2097184 | tf_op jit(solution)/shard_map/all_to_all | solution.py:263
  40.6 64.2 %all-gather = s32[8,1,128]{2,1,0:T(1,128)S(1)} all-gather(s32[1,1,128]{2,1,0:T(1,128)S(1)} %bitcast.29), channel_id=1, replica_groups=mesh['data'=2,'seq'=8] {'seq'}, dimensions={0}, use_global_device_ids=true | all-gather | bytes 4608 | tf_op jit(solution)/shard_map/all_gather | solution.py:271
  114.6 9.5 fusion.2.x_ref
  124.1 70.9 %qkv_project.3.q_ref.k_ref.v_ref = bf16[1536,9216]{1,0:T(8,128)(2,1)} custom-call(bf16[1536,2048]{1,0:T(8,128)(2,1)} %fusion.2.x_ref, bf16[3,2048,24,128]{3,2,1,0:T(8,128)(2,1)} %wq_ref.5, bf16[3,2048,24,128]{3,2,1,0:T(8,128)(2,1)} %wk_ref.5, bf16[3,2048,24,128]{3,2,1,0:T(8,128)(2,1)} %wv_ref.5, f32[1536,128]{1,0:T(8,128)} %get-tuple-element.36.cos_ref, ...), custom_call_target="tpu_custom_call" | custom-call | flops 57982058496 | bytes 37748736 | tf_op jit(solution)/shard_map/qkv_project/pallas_call | solution.py:53
  195.1 6.4 slice.55
  202.1 5.8 pad_maximum_fusion.x_ref
  207.9 41.8 %attend_whole.3.prev_ref = bf16[1536,3072]{1,0:T(8,128)(2,1)} custom-call(bf16[1536,9216]{1,0:T(8,128)(2,1)} %qkv_project.3.q_ref.k_ref.v_ref, bf16[1536,9216]{1,0:T(8,128)(2,1)} %qkv_project.3.q_ref.k_ref.v_ref, bf16[1536,9216]{1,0:T(8,128)(2,1)} %qkv_project.3.q_ref.k_ref.v_ref), custom_call_target="tpu_custom_call" | custom-call | flops 25769803776 | bytes 25165824 | tf_op jit(solution)/shard_map/attend_whole/pallas_call | solution.py:132
  249.7 23.7 %attend_half.3.o_ref = bf16[1536,3072]{1,0:T(8,128)(2,1)} custom-call(s32[1]{0:T(128)} %bitcast.core_ref, bf16[1536,9216]{1,0:T(8,128)(2,1)} %qkv_project.3.q_ref.k_ref.v_ref, bf16[1536,9216]{1,0:T(8,128)(2,1)} %qkv_project.3.q_ref.k_ref.v_ref, bf16[1536,9216]{1,0:T(8,128)(2,1)} %qkv_project.3.q_ref.k_ref.v_ref, ...), custom_call_target="tpu_custom_call", output_to_operand_aliasing={{}: (6, {})} | custom-call | flops 6442450944 | bytes 18874368 | tf_op jit(solution)/shard_map/attend_half/pallas_call | solution.py:147
  273.4 29.8 %out_project.3 = (bf16[1536,2048]{1,0:T(8,128)(2,1)}, bf16[1536,2048]{1,0:T(8,128)(2,1)}) custom-call(bf16[1536,3072]{1,0:T(8,128)(2,1)} %attend_half.3.o_ref, bf16[1536,2048]{1,0:T(8,128)(2,1)} %pad_maximum_fusion.x_ref, bf16[3,3072,2048]{2,1,0:T(8,128)(2,1)} %bitcast.30, f32[1,2048]{1,0:T(1,128)} %get-tuple-element.28.g_ref), custom_call_target="tpu_custom_call" | custom-call | flops 19327352832 | bytes 12582912 | tf_op jit(solution)/shard_map/out_project/pallas_call | solution.py:183
  303.2 128.7 %mlp.3 = (bf16[1536,2048]{1,0:T(8,128)(2,1)}, bf16[1536,2048]{1,0:T(8,128)(2,1)}) custom-call(bf16[1536,2048]{1,0:T(8,128)(2,1)} %get-tuple-element.16.r_ref, bf16[1536,2048]{1,0:T(8,128)(2,1)} %get-tuple-element.17.h_ref, bf16[3,2048,8192]{2,1,0:T(8,128)(2,1)} %up_ref.5, bf16[3,8192,2048]{2,1,0:T(8,128)(2,1)} %down_ref.5, f32[1,2048]{1,0:T(1,128)} %get-tuple-element.32.g_ref), custom_call_target="tpu_custom_call" | custom-call | flops 103079215104 | bytes 67108864 | tf_op jit(solution)/shard_map/mlp/pallas_call | solution.py:228
  432.0 71.1 %qkv_project.4.q_ref.k_ref.v_ref = bf16[1536,9216]{1,0:T(8,128)(2,1)} custom-call(bf16[1536,2048]{1,0:T(8,128)(2,1)} %get-tuple-element.18.x_ref, bf16[3,2048,24,128]{3,2,1,0:T(8,128)(2,1)} %wq_ref.5, bf16[3,2048,24,128]{3,2,1,0:T(8,128)(2,1)} %wk_ref.5, bf16[3,2048,24,128]{3,2,1,0:T(8,128)(2,1)} %wv_ref.5, f32[1536,128]{1,0:T(8,128)} %get-tuple-element.36.cos_ref, ...), custom_call_target="tpu_custom_call" | custom-call | flops 57982058496 | bytes 37748736 | tf_op jit(solution)/shard_map/qkv_project/pallas_call | solution.py:53
  503.0 6.2 slice.56
  509.8 41.8 %attend_whole.4.prev_ref = bf16[1536,3072]{1,0:T(8,128)(2,1)} custom-call(bf16[1536,9216]{1,0:T(8,128)(2,1)} %qkv_project.4.q_ref.k_ref.v_ref, bf16[1536,9216]{1,0:T(8,128)(2,1)} %qkv_project.4.q_ref.k_ref.v_ref, bf16[1536,9216]{1,0:T(8,128)(2,1)} %qkv_project.4.q_ref.k_ref.v_ref), custom_call_target="tpu_custom_call" | custom-call | flops 25769803776 | bytes 25165824 | tf_op jit(solution)/shard_map/attend_whole/pallas_call | solution.py:132
  551.6 23.7 %attend_half.4.o_ref = bf16[1536,3072]{1,0:T(8,128)(2,1)} custom-call(s32[1]{0:T(128)} %bitcast.core_ref, bf16[1536,9216]{1,0:T(8,128)(2,1)} %qkv_project.4.q_ref.k_ref.v_ref, bf16[1536,9216]{1,0:T(8,128)(2,1)} %qkv_project.4.q_ref.k_ref.v_ref, bf16[1536,9216]{1,0:T(8,128)(2,1)} %qkv_project.4.q_ref.k_ref.v_ref, ...), custom_call_target="tpu_custom_call", output_to_operand_aliasing={{}: (6, {})} | custom-call | flops 6442450944 | bytes 18874368 | tf_op jit(solution)/shard_map/attend_half/pallas_call | solution.py:147
  575.3 29.7 %out_project.4 = (bf16[1536,2048]{1,0:T(8,128)(2,1)}, bf16[1536,2048]{1,0:T(8,128)(2,1)}) custom-call(bf16[1536,3072]{1,0:T(8,128)(2,1)} %attend_half.4.o_ref, bf16[1536,2048]{1,0:T(8,128)(2,1)} %get-tuple-element.19.x_ref, bf16[3,3072,2048]{2,1,0:T(8,128)(2,1)} %bitcast.31, f32[1,2048]{1,0:T(1,128)} %get-tuple-element.29.g_ref), custom_call_target="tpu_custom_call" | custom-call | flops 19327352832 | bytes 12582912 | tf_op jit(solution)/shard_map/out_project/pallas_call | solution.py:183
  605.0 128.9 %mlp.4 = (bf16[1536,2048]{1,0:T(8,128)(2,1)}, bf16[1536,2048]{1,0:T(8,128)(2,1)}) custom-call(bf16[1536,2048]{1,0:T(8,128)(2,1)} %get-tuple-element.20.r_ref, bf16[1536,2048]{1,0:T(8,128)(2,1)} %get-tuple-element.21.h_ref, bf16[3,2048,8192]{2,1,0:T(8,128)(2,1)} %up_ref.5, bf16[3,8192,2048]{2,1,0:T(8,128)(2,1)} %down_ref.5, f32[1,2048]{1,0:T(1,128)} %get-tuple-element.30.g_ref), custom_call_target="tpu_custom_call" | custom-call | flops 103079215104 | bytes 67108864 | tf_op jit(solution)/shard_map/mlp/pallas_call | solution.py:228
  733.9 70.8 %qkv_project.5.q_ref.k_ref.v_ref = bf16[1536,9216]{1,0:T(8,128)(2,1)} custom-call(bf16[1536,2048]{1,0:T(8,128)(2,1)} %get-tuple-element.22.x_ref, bf16[3,2048,24,128]{3,2,1,0:T(8,128)(2,1)} %wq_ref.5, bf16[3,2048,24,128]{3,2,1,0:T(8,128)(2,1)} %wk_ref.5, bf16[3,2048,24,128]{3,2,1,0:T(8,128)(2,1)} %wv_ref.5, f32[1536,128]{1,0:T(8,128)} %get-tuple-element.36.cos_ref, ...), custom_call_target="tpu_custom_call" | custom-call | flops 57982058496 | bytes 37748736 | tf_op jit(solution)/shard_map/qkv_project/pallas_call | solution.py:53
  804.8 6.2 slice.57
  811.0 41.8 %attend_whole.5.prev_ref = bf16[1536,3072]{1,0:T(8,128)(2,1)} custom-call(bf16[1536,9216]{1,0:T(8,128)(2,1)} %qkv_project.5.q_ref.k_ref.v_ref, bf16[1536,9216]{1,0:T(8,128)(2,1)} %qkv_project.5.q_ref.k_ref.v_ref, bf16[1536,9216]{1,0:T(8,128)(2,1)} %qkv_project.5.q_ref.k_ref.v_ref), custom_call_target="tpu_custom_call" | custom-call | flops 25769803776 | bytes 25165824 | tf_op jit(solution)/shard_map/attend_whole/pallas_call | solution.py:132
  852.8 23.7 %attend_half.5.o_ref = bf16[1536,3072]{1,0:T(8,128)(2,1)} custom-call(s32[1]{0:T(128)} %bitcast.core_ref, bf16[1536,9216]{1,0:T(8,128)(2,1)} %qkv_project.5.q_ref.k_ref.v_ref, bf16[1536,9216]{1,0:T(8,128)(2,1)} %qkv_project.5.q_ref.k_ref.v_ref, bf16[1536,9216]{1,0:T(8,128)(2,1)} %qkv_project.5.q_ref.k_ref.v_ref, ...), custom_call_target="tpu_custom_call", output_to_operand_aliasing={{}: (6, {})} | custom-call | flops 6442450944 | bytes 18874368 | tf_op jit(solution)/shard_map/attend_half/pallas_call | solution.py:147
  876.5 29.7 %out_project.5 = (bf16[1536,2048]{1,0:T(8,128)(2,1)}, bf16[1536,2048]{1,0:T(8,128)(2,1)}) custom-call(bf16[1536,3072]{1,0:T(8,128)(2,1)} %attend_half.5.o_ref, bf16[1536,2048]{1,0:T(8,128)(2,1)} %get-tuple-element.23.x_ref, bf16[3,3072,2048]{2,1,0:T(8,128)(2,1)} %bitcast.32, f32[1,2048]{1,0:T(1,128)} %get-tuple-element.27.g_ref), custom_call_target="tpu_custom_call" | custom-call | flops 19327352832 | bytes 12582912 | tf_op jit(solution)/shard_map/out_project/pallas_call | solution.py:183
  906.3 129.1 %mlp.5 = (bf16[1536,2048]{1,0:T(8,128)(2,1)}, bf16[1536,2048]{1,0:T(8,128)(2,1)}) custom-call(bf16[1536,2048]{1,0:T(8,128)(2,1)} %get-tuple-element.24.r_ref, bf16[1536,2048]{1,0:T(8,128)(2,1)} %get-tuple-element.25.h_ref, bf16[3,2048,8192]{2,1,0:T(8,128)(2,1)} %up_ref.5, bf16[3,8192,2048]{2,1,0:T(8,128)(2,1)} %down_ref.5, f32[1,2048]{1,0:T(1,128)} %get-tuple-element.30.g_ref), custom_call_target="tpu_custom_call" | custom-call | flops 103079215104 | bytes 67108864 | tf_op jit(solution)/shard_map/mlp/pallas_call | solution.py:228
  1047.2 22.2 %all-to-all-done.3 = bf16[8,64,2048]{2,1,0:T(8,128)(2,1)S(1)} async-done(((bf16[8,64,2048]{2,1,0:T(8,128)(2,1)}), bf16[8,64,2048]{2,1,0:T(8,128)(2,1)S(1)}, u32[]{:S(2)}, u32[]{:S(2)}) %all-to-all-start.3) | async-done | bytes 2097184 | tf_op jit(solution)/shard_map/all_to_all | solution.py:263
  1069.3 53.3 %all_to_all.20 = bf16[8,128,2048]{2,1,0:T(8,128)(2,1)S(1)} all-to-all(bf16[8,128,2048]{2,1,0:T(8,128)(2,1)} %bitcast.22), channel_id=1, replica_groups=mesh['data'=2,'seq'=8] {'seq'}, dimensions={0} | all-to-all | bytes 8388608 | tf_op jit(solution)/shard_map/all_to_all | solution.py:263
  (38 shorter events, 44.1 us)
Async XLA Ops:
  3.2 32.5 %all-to-all-start.1 = ((bf16[8,64,2048]{2,1,0:T(8,128)(2,1)}), bf16[8,64,2048]{2,1,0:T(8,128)(2,1)S(1)}, u32[]{:S(2)}, u32[]{:S(2)}) async-start(bf16[8,64,2048]{2,1,0:T(8,128)(2,1)} %bitcast.23), calls=%async_computation.1 | async-start | bytes 4194304 | tf_op jit(solution)/shard_map/all_to_all | solution.py:263
  13.3 27.3 %copy-start.4 = (s32[128]{0:T(128)S(1)}, s32[128]{0:T(128)}, u32[]{:S(2)}) copy-start(s32[128]{0:T(128)} %param.11) | copy-start | bytes 1540
  35.7 78.9 %copy-start = (bf16[8,64,2048]{2,1,0:T(8,128)(2,1)}, bf16[8,64,2048]{2,1,0:T(8,128)(2,1)S(1)}, u32[]{:S(2)}) copy-start(bf16[8,64,2048]{2,1,0:T(8,128)(2,1)S(1)} %all-to-all-done.1) | copy-start | bytes 6291460
  35.7 74.8 %copy-start.2 = (f32[3,2048]{1,0:T(4,128)S(1)}, f32[3,2048]{1,0:T(4,128)}, u32[]{:S(2)}) copy-start(f32[3,2048]{1,0:T(4,128)} %param.18) | copy-start | bytes 73732
  35.7 75.4 %all-to-all-start = ((bf16[8,128,2048]{2,1,0:T(8,128)(2,1)}), bf16[8,128,2048]{2,1,0:T(8,128)(2,1)}, u32[]{:S(2)}, u32[]{:S(2)}) async-start(bf16[8,128,2048]{2,1,0:T(8,128)(2,1)} %bitcast.21), calls=%async_computation | async-start | bytes 8388608 | tf_op jit(solution)/shard_map/all_to_all | solution.py:263
  195.1 6.4 copy-start.3
  195.1 7.0 copy-start.1
  201.5 48.3 %collective-permute-start = (bf16[512,6144]{1,0:T(8,128)(2,1)}, bf16[512,6144]{1,0:T(8,128)(2,1)}, u32[]{:S(2)}, u32[]{:S(2)}) collective-permute-start(bf16[512,6144]{1,0:T(8,128)(2,1)} %slice.55), channel_id=1, source_target_pairs={{0,1},{1,0},{2,3},{3,2},{4,5},{5,4},{6,7},{7,6},{8,9},{9,8},{10,11... | collective-permute-start | bytes 18874376 | tf_op jit(solution)/shard_map/ppermute | solution.py:284
  509.3 42.3 %collective-permute-start.1 = (bf16[512,6144]{1,0:T(8,128)(2,1)}, bf16[512,6144]{1,0:T(8,128)(2,1)}, u32[]{:S(2)}, u32[]{:S(2)}) collective-permute-start(bf16[512,6144]{1,0:T(8,128)(2,1)} %slice.56), channel_id=1, source_target_pairs={{0,1},{1,0},{2,3},{3,2},{4,5},{5,4},{6,7},{7,6},{8,9},{9,8},{10,11... | collective-permute-start | bytes 18874376 | tf_op jit(solution)/shard_map/ppermute | solution.py:284
  811.0 41.8 %collective-permute-start.2 = (bf16[512,6144]{1,0:T(8,128)(2,1)}, bf16[512,6144]{1,0:T(8,128)(2,1)}, u32[]{:S(2)}, u32[]{:S(2)}) collective-permute-start(bf16[512,6144]{1,0:T(8,128)(2,1)} %slice.57), channel_id=1, source_target_pairs={{0,1},{1,0},{2,3},{3,2},{4,5},{5,4},{6,7},{7,6},{8,9},{9,8},{10,11... | collective-permute-start | bytes 18874376 | tf_op jit(solution)/shard_map/ppermute | solution.py:284
  1038.6 30.8 %all-to-all-start.3 = ((bf16[8,64,2048]{2,1,0:T(8,128)(2,1)}), bf16[8,64,2048]{2,1,0:T(8,128)(2,1)S(1)}, u32[]{:S(2)}, u32[]{:S(2)}) async-start(bf16[8,64,2048]{2,1,0:T(8,128)(2,1)} %bitcast.12), calls=%async_computation.3 | async-start | bytes 4194304 | tf_op jit(solution)/shard_map/all_to_all | solution.py:263

commit v2 on v1

v2 whole, which is shorter than its diff:
```python
import functools

import jax
import jax.numpy as jnp
from jax import lax
from jax.experimental import pallas as pl
from jax.experimental.pallas import tpu as pltpu
from jax.sharding import PartitionSpec as P

ROPE_BASE = 10000.0
NORM_EPS = 1e-6
MASKED = -1e30
VMEM_LIMIT = 62 * 2**20


def norm_rows(x_f32, gain_row):
    mean_sq = jnp.mean(x_f32 * x_f32, axis=-1, keepdims=True)
    return (x_f32 * lax.rsqrt(mean_sq + NORM_EPS) * gain_row).astype(jnp.bfloat16)


def flat(ref, lo, n):
    return ref[lo : lo + n].reshape(n * ref.shape[1], ref.shape[2])


def project_steps(steps, group, get_x, wq_ref, wk_ref, wv_ref, cos_ref, sin_ref, out_ref, kv_ref, kv_lo):
    step = pl.program_id(0)
    groups, per_group = out_ref.shape[:2]
    depth, hb, dh = wq_ref.shape

    def project(w_ref, rotate, keep):
        w = w_ref[...].reshape(depth, hb * dh)
        for lo in range(0, groups, group):
            here = slice(lo, lo + group)
            acc = jnp.dot(get_x(lo, group), w, preferred_element_type=jnp.float32)
            if rotate:
                cos, sin = flat(cos_ref, lo, group), flat(sin_ref, lo, group)
                for h in range(hb):
                    cols = slice(h * dh, (h + 1) * dh)
                    u = acc[:, cols]
                    rot = (u * cos + pltpu.roll(u, dh // 2, 1) * sin).astype(jnp.bfloat16)
                    out_ref[here, :, cols] = rot.reshape(group, per_group, dh)
            else:
                out_ref[here] = acc.astype(jnp.bfloat16).reshape(group, per_group, hb * dh)
        if keep and kv_ref is not None:
            kv_ref[...] = out_ref[:, kv_lo:, :]

    pl.when(step < steps)(lambda: project(wq_ref, True, False))
    pl.when((step >= steps) & (step < 2 * steps))(lambda: project(wk_ref, True, True))
    pl.when(step >= 2 * steps)(lambda: project(wv_ref, False, True))


def later_kernel(steps, group, kv_lo, x_ref, wq_ref, wk_ref, wv_ref, cos_ref, sin_ref, out_ref, kv_ref):
    get_x = lambda lo, n: flat(x_ref, lo, n)
    project_steps(steps, group, get_x, wq_ref, wk_ref, wv_ref, cos_ref, sin_ref, out_ref, kv_ref, kv_lo)


def first_kernel(steps, with_kv, n_prev, x_ref, g_ref, wq_ref, wk_ref, wv_ref, cos_ref, sin_ref, *refs):
    out_ref, hid_ref = refs[n_prev : n_prev + 2]
    kv_ref = refs[n_prev + 2] if with_kv else None
    xn_ref = refs[-1]

    @pl.when(pl.program_id(0) == 0)
    def _():
        x = x_ref[...]
        hid_ref[...] = x
        xn_ref[...] = norm_rows(x.reshape(xn_ref.shape).astype(jnp.float32), g_ref[...])

    get_x = lambda lo, n: xn_ref[...]
    project_steps(steps, x_ref.shape[0], get_x, wq_ref, wk_ref, wv_ref, cos_ref, sin_ref, out_ref, kv_ref, 0)


def weight_specs(w, layer, hb):
    depth, heads, dh = w.shape[1:]
    steps = heads // hb
    pick = lambda part: pl.BlockSpec(
        (None, depth, hb, dh), lambda i: (layer, 0, jnp.clip(i - part * steps, 0, steps - 1), 0)
    )
    return [pick(0), pick(1), pick(2)], steps


def qkv_cost(rows, w):
    n = w.shape[1] * w.shape[2] * w.shape[3]
    return pl.CostEstimate(flops=6 * rows * n, bytes_accessed=6 * n, transcendentals=0)


def qkv_first(x_part, part, prev, w_query, w_key, w_value, cos, sin, gain, with_kv):
    shards, piece, depth = x_part.shape
    per_shard = cos.shape[1]
    heads, dh = w_query.shape[2:]
    hb = 8
    w_specs, steps = weight_specs(w_query, 0, hb)
    kv_block = lambda i: (0, 0, jnp.clip(i - steps, 0, 2 * steps - 1))
    whole = lambda shape: pl.BlockSpec(shape, lambda i: (0,) * len(shape))
    here = lambda n: pl.BlockSpec((shards, piece, n), lambda i: (0, part, 0))
    out_specs = [pl.BlockSpec((shards, piece, hb * dh), lambda i: (0, part, i)), here(depth)]
    out_shape = [
        jax.ShapeDtypeStruct((shards, per_shard, 3 * heads * dh), jnp.bfloat16),
        jax.ShapeDtypeStruct((shards, per_shard, depth), jnp.bfloat16),
    ]
    if with_kv:
        out_specs.append(pl.BlockSpec((shards, piece, hb * dh), kv_block))
        out_shape.append(jax.ShapeDtypeStruct((shards, piece, 2 * heads * dh), jnp.bfloat16))
    return pl.pallas_call(
        functools.partial(first_kernel, steps, with_kv, len(prev)),
        grid=(3 * steps,),
        in_specs=[whole((shards, piece, depth)), whole((1, depth)), *w_specs, here(dh), here(dh)]
        + [pl.BlockSpec(memory_space=pl.ANY)] * len(prev),
        out_specs=out_specs,
        out_shape=out_shape,
        input_output_aliases={7 + i: i for i in range(len(prev))},
        scratch_shapes=[pltpu.VMEM((shards * piece, depth), jnp.bfloat16)],
        compiler_params=pltpu.CompilerParams(vmem_limit_bytes=VMEM_LIMIT),
        cost_estimate=qkv_cost(shards * piece, w_query),
        name="qkv_first",
    )(x_part, gain, w_query, w_key, w_value, cos, sin, *prev)


def qkv_later(x, w_query, w_key, w_value, cos, sin, layer, piece):
    shards, per_shard, depth = x.shape
    heads, dh = w_query.shape[2:]
    hb = 8
    w_specs, steps = weight_specs(w_query, layer, hb)
    kv_block = lambda i: (0, 0, jnp.clip(i - steps, 0, 2 * steps - 1))
    whole = lambda shape: pl.BlockSpec(shape, lambda i: (0,) * len(shape))
    return pl.pallas_call(
        functools.partial(later_kernel, steps, shards // 2, per_shard - piece),
        grid=(3 * steps,),
        in_specs=[whole(x.shape), *w_specs, whole(cos.shape), whole(sin.shape)],
        out_specs=[
            pl.BlockSpec((shards, per_shard, hb * dh), lambda i: (0, 0, i)),
            pl.BlockSpec((shards, piece, hb * dh), kv_block),
        ],
        out_shape=[
            jax.ShapeDtypeStruct((shards, per_shard, 3 * heads * dh), jnp.bfloat16),
            jax.ShapeDtypeStruct((shards, piece, 2 * heads * dh), jnp.bfloat16),
        ],
        compiler_params=pltpu.CompilerParams(vmem_limit_bytes=VMEM_LIMIT),
        cost_estimate=qkv_cost(shards * per_shard, w_query),
        name="qkv_later",
    )(x, w_query, w_key, w_value, cos, sin)


def scores(q, k):
    return lax.dot_general(q, k, (((1,), (1,)), ((), ())), preferred_element_type=jnp.float32)


def softmax_sum(score_list, value_list, scale2):
    row_max = functools.reduce(jnp.maximum, [jnp.max(s, axis=-1, keepdims=True) for s in score_list])
    offset = row_max * scale2
    exps = [jnp.exp2(s * scale2 - offset) for s in score_list]
    row_sum = sum(jnp.sum(e, axis=-1, keepdims=True) for e in exps)
    out = sum(
        jnp.dot(e.astype(jnp.bfloat16), v, preferred_element_type=jnp.float32) for e, v in zip(exps, value_list)
    )
    return (out * (1.0 / row_sum)).astype(jnp.bfloat16)


def run_tiles(n_heads, n_tiles, get_scores, finish):
    order = [(h, t if h % 2 == 0 else n_tiles - 1 - t) for h in range(n_heads) for t in range(n_tiles)]
    held = get_scores(*order[0])
    for pos, task in enumerate(order):
        ahead = get_scores(*order[pos + 1]) if pos + 1 < len(order) else None
        finish(*task, held)
        held = ahead


def whole_kernel(tile, scale2, dh, q_ref, k_ref, v_ref, out_ref):
    shards, per, width = q_ref.shape
    gt = tile // per
    causal = lax.broadcasted_iota(jnp.int32, (tile, tile), 1) <= lax.broadcasted_iota(jnp.int32, (tile, tile), 0)
    part = lambda ref, lo, n, h: ref[lo : lo + n, :, h * dh : (h + 1) * dh].reshape(n * per, dh)

    def get_scores(h, t):
        q = part(q_ref, t * gt, gt, h)
        s = scores(q, part(k_ref, 0, (t + 1) * gt, h))
        last = jnp.where(causal, s[:, t * tile :], MASKED)
        return [s[:, : t * tile], last] if t else [last]

    def finish(h, t, held):
        values = [part(v_ref, 0, t * gt, h)] if t else []
        values.append(part(v_ref, t * gt, gt, h))
        out = softmax_sum(held, values, scale2)
        out_ref[t * gt : (t + 1) * gt, :, h * dh : (h + 1) * dh] = out.reshape(gt, per, dh)

    run_tiles(width // dh, shards // gt, get_scores, finish)


def half_kernel(tile, scale2, dh, core_ref, q_ref, k_ref, v_ref, k2_ref, v2_ref, prev_ref, out_ref):
    shards, piece, width = q_ref.shape
    gt = tile // piece
    core = core_ref[0]
    key = lax.broadcasted_iota(jnp.int32, (tile, tile), 1)
    query = lax.broadcasted_iota(jnp.int32, (tile, tile), 0)
    causal = key <= query
    causal2 = key // piece < query // piece + core
    part = lambda ref, lo, n, h: ref[lo : lo + n, :, h * dh : (h + 1) * dh].reshape(n * piece, dh)

    def get_scores(h, t):
        q = part(q_ref, t * gt, gt, h)
        out = []
        for ref, mask in ((k_ref, causal), (k2_ref, causal2)):
            s = scores(q, part(ref, 0, (t + 1) * gt, h))
            out += [s[:, : t * tile]] if t else []
            out.append(jnp.where(mask, s[:, t * tile :], MASKED))
        return out

    def finish(h, t, held):
        values = []
        for ref in (v_ref, v2_ref):
            values += [part(ref, 0, t * gt, h)] if t else []
            values.append(part(ref, t * gt, gt, h))
        out = softmax_sum(held, values, scale2)
        out_ref[t * gt : (t + 1) * gt, :, h * dh : (h + 1) * dh] = out.reshape(gt, piece, dh)

    run_tiles(width // dh, shards // gt, get_scores, finish)


def attention(qkv, kv_own, kv_other, core, heads, dh):
    shards, per_shard = qkv.shape[:2]
    piece = kv_own.shape[1]
    n_whole, n_half = shards * 2 * piece, shards * piece
    tile = 256
    scale2 = float(dh**-0.5 * 1.4426950408889634)
    group = 2
    width = group * dh
    steps = heads // group
    params = pltpu.CompilerParams(vmem_limit_bytes=VMEM_LIMIT)
    out_shape = jax.ShapeDtypeStruct((shards, per_shard, heads * dh), jnp.bfloat16)
    whole = lambda third: pl.BlockSpec((shards, 2 * piece, width), lambda h: (0, 0, third * steps + h))
    out = pl.pallas_call(
        functools.partial(whole_kernel, tile, scale2, dh),
        grid=(steps,),
        in_specs=[whole(0), whole(1), whole(2)],
        out_specs=whole(0),
        out_shape=out_shape,
        compiler_params=params,
        cost_estimate=pl.CostEstimate(
            flops=8 * n_whole * n_whole * heads * dh, bytes_accessed=8 * n_whole * heads * dh, transcendentals=0
        ),
        name="attend_whole",
    )(qkv, qkv, qkv)
    shared = pl.BlockSpec((shards, piece, width), lambda h: (0, 2, h))
    side = lambda second: pl.BlockSpec((shards, piece, width), lambda h: (0, 0, second * steps + h))
    return pl.pallas_call(
        functools.partial(half_kernel, tile, scale2, dh),
        grid=(steps,),
        in_specs=[
            pl.BlockSpec(memory_space=pltpu.SMEM),
            shared,
            side(0),
            side(1),
            side(0),
            side(1),
            pl.BlockSpec(memory_space=pl.ANY),
        ],
        out_specs=shared,
        out_shape=out_shape,
        input_output_aliases={6: 0},
        compiler_params=params,
        cost_estimate=pl.CostEstimate(
            flops=8 * n_half * n_half * heads * dh, bytes_accessed=12 * n_half * heads * dh, transcendentals=0
        ),
        name="attend_half",
    )(core, qkv, kv_own, kv_own, kv_other, kv_other, out)


def out_kernel(sub, o_ref, x_ref, w_ref, g_ref, h_ref, r_ref, acc):
    k, m = pl.program_id(0), pl.program_id(1)
    last = pl.num_programs(0) - 1
    rows = o_ref.shape[0]
    dot = lambda r: jnp.dot(o_ref[r : r + sub, :], w_ref[...], preferred_element_type=jnp.float32)

    @pl.when(k == 0)
    def _():
        for r in range(0, rows, sub):
            acc[m, r : r + sub, :] = dot(r)

    @pl.when((k > 0) & (k < last))
    def _():
        for r in range(0, rows, sub):
            acc[m, r : r + sub, :] += dot(r)

    @pl.when(k == last)
    def _():
        held = dot(0)
        for r in range(0, rows, sub):
            ahead = dot(r + sub) if r + sub < rows else None
            h = (x_ref[r : r + sub, :].astype(jnp.float32) + (acc[m, r : r + sub, :] + held)).astype(jnp.bfloat16)
            h_ref[r : r + sub, :] = h
            r_ref[r : r + sub, :] = norm_rows(h.astype(jnp.float32), g_ref[...])
            held = ahead


def out_project(o, x, w_out, gain, layer):
    rows, depth = o.shape
    width = x.shape[1]
    mb, tk = 512, depth // 2
    at_end = pl.BlockSpec((mb, width), lambda k, m: (jnp.where(k == depth // tk - 1, m, 0), 0))
    return pl.pallas_call(
        functools.partial(out_kernel, 256),
        grid=(depth // tk, rows // mb),
        in_specs=[
            pl.BlockSpec((mb, tk), lambda k, m: (m, k)),
            at_end,
            pl.BlockSpec((None, tk, width), lambda k, m: (layer, k, 0)),
            pl.BlockSpec((1, width), lambda k, m: (0, 0)),
        ],
        out_specs=[at_end] * 2,
        out_shape=[jax.ShapeDtypeStruct((rows, width), jnp.bfloat16)] * 2,
        scratch_shapes=[pltpu.VMEM((rows // mb, mb, width), jnp.float32)],
        compiler_params=pltpu.CompilerParams(vmem_limit_bytes=VMEM_LIMIT),
        cost_estimate=pl.CostEstimate(
            flops=2 * rows * depth * width, bytes_accessed=2 * depth * width, transcendentals=0
        ),
        name="out_project",
    )(o, x, w_out, gain)


def mlp_kernel(group, r_ref, h_ref, up_ref, down_ref, *refs):
    g_ref, y_ref, n_ref, acc = refs if len(refs) == 4 else (None, refs[0], None, refs[1])
    f = pl.program_id(1)
    groups, per, width = r_ref.shape
    sub = group * per
    up = lambda lo: jnp.dot(flat(r_ref, lo, group), up_ref[...], preferred_element_type=jnp.float32)

    def add_block(first):
        held = up(0)
        for lo in range(0, groups, group):
            ahead = up(lo + group) if lo + group < groups else None
            z = jax.nn.gelu(held, approximate=True).astype(jnp.bfloat16)
            prod = jnp.dot(z, down_ref[...], preferred_element_type=jnp.float32)
            rows = slice(lo * per, lo * per + sub)
            if first:
                acc[rows, :] = prod
            else:
                acc[rows, :] += prod
            held = ahead

    pl.when(f == 0)(lambda: add_block(True))
    pl.when(f > 0)(lambda: add_block(False))

    @pl.when(f == pl.num_programs(1) - 1)
    def _():
        for lo in range(groups):
            rows = slice(lo * per, (lo + 1) * per)
            y = (h_ref[lo].astype(jnp.float32) + acc[rows, :]).astype(jnp.bfloat16)
            y_ref[lo] = y
            if n_ref is not None:
                n_ref[lo] = norm_rows(y.astype(jnp.float32), g_ref[...])


def mlp(r, h, w_up, w_down, gain, layer, part=None, piece=None):
    shards, per_shard, width = r.shape
    ff = w_up.shape[2]
    tf = 1024
    if part is None:
        blocks, block = 2, (shards // 2, per_shard, width)
        group = shards // 4
        in_row = out_row = pl.BlockSpec(block, lambda m, f: (m, 0, 0))
        extra, extra_specs = [gain], [pl.BlockSpec((1, width), lambda m, f: (0, 0))]
        out_shape = [jax.ShapeDtypeStruct(r.shape, jnp.bfloat16)] * 2
    else:
        blocks, block = 1, (shards, piece, width)
        group = shards // 2
        in_row = pl.BlockSpec(block, lambda m, f: (0, part, 0))
        out_row = pl.BlockSpec(block, lambda m, f: (0, 0, 0))
        extra, extra_specs = [], []
        out_shape = [jax.ShapeDtypeStruct(block, jnp.bfloat16)]
    rows = blocks * block[0] * block[1]
    return pl.pallas_call(
        functools.partial(mlp_kernel, group),
        grid=(blocks, ff // tf),
        in_specs=[
            in_row,
            in_row,
            pl.BlockSpec((None, width, tf), lambda m, f: (layer, 0, f)),
            pl.BlockSpec((None, tf, width), lambda m, f: (layer, f, 0)),
            *extra_specs,
        ],
        out_specs=[out_row] * len(out_shape),
        out_shape=out_shape,
        scratch_shapes=[pltpu.VMEM((block[0] * block[1], width), jnp.float32)],
        compiler_params=pltpu.CompilerParams(vmem_limit_bytes=VMEM_LIMIT),
        cost_estimate=pl.CostEstimate(
            flops=4 * rows * ff * width, bytes_accessed=4 * ff * width, transcendentals=0
        ),
        name="mlp",
    )(r, h, w_up, w_down, *extra)


def solution(mesh):
    n_seq = mesh.shape["seq"]
    n_pair = n_seq // 2
    tok_spec = P(None, ("data", "seq"), None)
    in_specs = (tok_spec, P(("data", "seq"))) + (P(),) * 8
    partner = [(i, i ^ 1) for i in range(n_seq)]

    def device_fn(x_loc, pos_loc, w_query, w_key, w_value, w_out, w_up, w_down, g_attn, g_mlp):
        n_layers, _, heads, dh = w_query.shape
        n_batch, shard, width = x_loc.shape
        per = n_batch // n_pair
        assert per * n_pair == n_batch and per == 3
        piece = shard // 2
        core = lax.rem(lax.axis_index("seq"), 2)
        exchange = lambda a: lax.all_to_all(a, "seq", 0, 0, tiled=True)

        pos = lax.all_gather(pos_loc, "seq", tiled=True).reshape(n_seq, shard)
        by_chip = x_loc.reshape(n_pair, per, shard, width)
        sends = [by_chip[:, :2, i * piece : (i + 1) * piece].reshape(n_seq, piece, width) for i in range(2)]
        first, pos = lax.optimization_barrier((by_chip[:, 2].reshape(n_seq, piece, width), pos))
        shared_x = exchange(first)
        shared_x, send0 = lax.optimization_barrier((shared_x, sends[0]))
        x0 = exchange(send0)
        x0, send1 = lax.optimization_barrier((x0, sends[1]))
        x1 = exchange(send1)

        pos_shared = lax.dynamic_index_in_dim(pos.reshape(n_seq, 2, piece), core, axis=1, keepdims=False)
        inv_freq = ROPE_BASE ** (-jnp.arange(dh // 2, dtype=jnp.float32) * (2.0 / dh))
        angles = jnp.concatenate([pos, pos_shared], axis=1).astype(jnp.float32)[..., None] * inv_freq
        cos, sin = jnp.cos(angles), jnp.sin(angles)
        cos = jnp.concatenate([cos, cos], axis=-1)
        sin = jnp.concatenate([-sin, sin], axis=-1)
        core_arr = core.astype(jnp.int32).reshape(1)
        w_out2 = w_out.reshape(n_layers, heads * dh, width)
        flat2 = lambda a: a.reshape(-1, a.shape[-1])

        first_args = (w_query, w_key, w_value, cos, sin, g_attn[0][None])
        qkv, hidden, kv_own = qkv_first(shared_x, 2, [], *first_args, True)
        qkv, hidden = qkv_first(x0, 0, [qkv, hidden], *first_args, False)
        qkv, hidden = qkv_first(x1, 1, [qkv, hidden], *first_args, False)
        for layer in range(n_layers):
            if layer:
                qkv, kv_own = qkv_later(normed, w_query, w_key, w_value, cos, sin, layer, piece)
            kv_other = lax.ppermute(kv_own, "seq", partner)
            attn = attention(qkv, kv_own, kv_other, core_arr, heads, dh)
            resid, r = out_project(flat2(attn), flat2(hidden), w_out2, g_mlp[layer][None], layer)
            resid, r = resid.reshape(hidden.shape), r.reshape(hidden.shape)
            if layer < n_layers - 1:
                hidden, normed = mlp(r, resid, w_up, w_down, g_attn[layer + 1][None], layer)

        parts = []
        for part in range(3):
            (y,) = mlp(r, resid, w_up, w_down, None, n_layers - 1, part, piece)
            parts.append(exchange(y))
        whole = jnp.concatenate([a.reshape(n_pair, 2, piece, width) for a in parts[:2]], axis=2)
        shared = parts[2].reshape(n_pair, 1, shard, width)
        return jnp.concatenate([whole, shared], axis=1).reshape(n_batch, shard, width)

    return jax.shard_map(device_fn, mesh=mesh, in_specs=in_specs, out_specs=tok_spec, check_vma=False)
```

time: 1140 us -> 977 us (0.86)
  blocking collectives: 117 us -> 56.1 us
  Pallas kernels: 885 us -> 847 us
  local copies, waits for them, and re-layouts: 36.7 us -> 9.28 us
  waiting for transfers between devices: 44.6 us -> 18.6 us
  other arithmetic: 27.1 us -> 10.4 us
    pallas_call x3, Pallas kernels: 125 us -> 80.3 us  [attention(): pl.pallas_call(functools.partial(whole_kernel, tile, scale2, dh), grid=(s...]
    all_gather x1, blocking collectives: 64.2 us -> 24.2 us  [device_fn(): pos = lax.all_gather(pos_loc, 'seq', tiled=True).reshape(n_seq, shard)]
    slice x9 -> x4, local copies, waits for them, and re-layouts: 36 us -> 9.18 us  [the longest x1 4.79 us: device_fn(): by_chip[:, :2, i * piece:(i + 1) * piece].reshape(n_seq, piece, width)]
    all_to_all x3 -> x5, waiting for transfers between devices: 44.6 us -> 18.6 us  [device_fn(): exchange = lambda a: lax.all_to_all(a, 'seq', 0, 0, tiled=True)]
    all_to_all x1, blocking collectives: 53.3 us -> 31.9 us  [device_fn(): exchange = lambda a: lax.all_to_all(a, 'seq', 0, 0, tiled=True)]
    all_to_all x3 -> x5, starting transfers between devices: 14 us -> 24.7 us  [device_fn(): exchange = lambda a: lax.all_to_all(a, 'seq', 0, 0, tiled=True)]
    pallas_call x12 -> x16, Pallas kernels: 760 us -> 767 us  [the longest x5 383 us: mlp(): pl.pallas_call(functools.partial(mlp_kernel, group), grid=(blocks, ff //...]
  transfers between devices with their start and end apart: 6 -> 8, of which waited for: 2 -> 1; matrix products, arithmetic and copies ran while one was open for 2% -> 1% of each run, Pallas kernels for 11% -> 28%
where the time goes in v2:
time: 977 us; the launch traced here: 967 us
  Pallas kernels  847 us (87%)
  blocking collectives  56.1 us (6%)
  starting transfers between devices  25.6 us (3%)
  waiting for transfers between devices  18.6 us (2%)
  other arithmetic  10.4 us (1%)
    pallas_call x5, Pallas kernels, mlp(): pl.pallas_call(functools.partial(mlp_kernel, group), grid=(blocks, ff //...  383 us
    pallas_call x2, Pallas kernels, qkv_later(): pl.pallas_call(functools.partial(later_kernel, steps, shards // 2, per_sh...  145 us
    pallas_call x3, Pallas kernels, qkv_first(): pl.pallas_call(functools.partial(first_kernel, steps, with_kv, len(prev))...  95 us
    pallas_call x3, Pallas kernels, out_project(): pl.pallas_call(functools.partial(out_kernel, 256), grid=(depth // tk, row...  85.6 us
    pallas_call x3, Pallas kernels, attention(): pl.pallas_call(functools.partial(whole_kernel, tile, scale2, dh), grid=(s...  80.3 us
    pallas_call x3, Pallas kernels, attention(): pl.pallas_call(functools.partial(half_kernel, tile, scale2, dh), grid=(st...  58.1 us
    all_to_all x1, blocking collectives, device_fn(): exchange = lambda a: lax.all_to_all(a, 'seq', 0, 0, tiled=True)  31.9 us
    all_to_all x5, starting transfers between devices, device_fn(): exchange = lambda a: lax.all_to_all(a, 'seq', 0, 0, tiled=True)  24.7 us
  transfers between devices with their start and end apart: 8, of which 1 were waited for; matrix products, arithmetic and copies ran while one was open for 1% of the time, Pallas kernels for 28%

profile of v2, /device:TPU:112, one launch (start us, length us, event | category | flops | bytes accessed | tf_op | source)
XLA Modules:
  0.0 967.3 jit_solution(9674030518051771246)
XLA Ops:
  3.2 24.2 %all-gather = s32[8,1,128]{2,1,0:T(1,128)S(1)} all-gather(s32[1,1,128]{2,1,0:T(1,128)} %bitcast.46), channel_id=1, replica_groups=mesh['data'=2,'seq'=8] {'seq'}, dimensions={0}, use_global_device_ids=true | all-gather | bytes 4608 | tf_op jit(solution)/shard_map/all_gather | solution.py:407
  40.3 18.6 %all-to-all-done.x_ref = bf16[8,64,2048]{2,1,0:T(8,128)(2,1)} async-done(((bf16[8,64,2048]{2,1,0:T(8,128)(2,1)}), bf16[8,64,2048]{2,1,0:T(8,128)(2,1)}, u32[]{:S(2)}, u32[]{:S(2)}) %all-to-all-start) | async-done | bytes 2097184 | tf_op jit(solution)/shard_map/all_to_all | solution.py:405
  65.1 32.5 %qkv_first.3 = (bf16[8,192,9216]{2,1,0:T(8,128)(2,1)}, bf16[8,192,2048]{2,1,0:T(8,128)(2,1)}, bf16[8,64,6144]{2,1,0:T(8,128)(2,1)}) custom-call(bf16[8,64,2048]{2,1,0:T(8,128)(2,1)} %all-to-all-done.x_ref, f32[1,2048]{1,0:T(1,128)} %get-tuple-element.65.g_ref, bf16[3,2048,24,128]{3,2,1,0:T(8,128)(2,1)} %wq_ref.9, bf16[3,2048,24,128]{3,2,1,0:T(8,128)(2,1)} %wk_ref.9, ...), custom_call_target="tpu_custom_call" | custom-call | flops 19327352832 | bytes 37748736 | tf_op jit(solution)/shard_map/qkv_first/pallas_call | solution.py:103
  103.6 31.2 %qkv_first.4 = (bf16[8,192,9216]{2,1,0:T(8,128)(2,1)}, bf16[8,192,2048]{2,1,0:T(8,128)(2,1)}) custom-call(bf16[8,64,2048]{2,1,0:T(8,128)(2,1)} %all-to-all-done.1.x_ref, f32[1,2048]{1,0:T(1,128)} %get-tuple-element.65.g_ref, bf16[3,2048,24,128]{3,2,1,0:T(8,128)(2,1)} %wq_ref.9, ...), custom_call_target="tpu_custom_call", output_to_operand_aliasing={{0}: (7, {}), {1}: (8, {})} | custom-call | flops 19327352832 | bytes 37748736 | tf_op jit(solution)/shard_map/qkv_first/pallas_call | solution.py:103
  134.8 31.3 %qkv_first.5 = (bf16[8,192,9216]{2,1,0:T(8,128)(2,1)}, bf16[8,192,2048]{2,1,0:T(8,128)(2,1)}) custom-call(bf16[8,64,2048]{2,1,0:T(8,128)(2,1)} %all-to-all-done.2.x_ref, f32[1,2048]{1,0:T(1,128)} %get-tuple-element.65.g_ref, bf16[3,2048,24,128]{3,2,1,0:T(8,128)(2,1)} %wq_ref.9, ...), custom_call_target="tpu_custom_call", output_to_operand_aliasing={{0}: (7, {}), {1}: (8, {})} | custom-call | flops 19327352832 | bytes 37748736 | tf_op jit(solution)/shard_map/qkv_first/pallas_call | solution.py:103
  166.1 26.8 %attend_whole.3.prev_ref = bf16[8,192,3072]{2,1,0:T(8,128)(2,1)} custom-call(bf16[8,192,9216]{2,1,0:T(8,128)(2,1)} %get-tuple-element.42.q_ref.k_ref.v_ref, bf16[8,192,9216]{2,1,0:T(8,128)(2,1)} %get-tuple-element.42.q_ref.k_ref.v_ref, bf16[8,192,9216]{2,1,0:T(8,128)(2,1)} %get-tuple-element.42.q_ref.k_ref.v_ref), custom_call_target="tpu_custom_call" | custom-call | flops 25769803776 | bytes 25165824 | tf_op jit(solution)/shard_map/attend_whole/pallas_call | solution.py:230
  192.9 19.4 %attend_half.3 = bf16[8,192,3072]{2,1,0:T(8,128)(2,1)} custom-call(s32[1]{0:T(128)} %bitcast.core_ref, bf16[8,192,9216]{2,1,0:T(8,128)(2,1)} %get-tuple-element.42.q_ref.k_ref.v_ref, bf16[8,64,6144]{2,1,0:T(8,128)(2,1)} %get-tuple-element.43.k_ref.v_ref, bf16[8,64,6144]{2,1,0:T(8,128)(2,1)} %get-tuple-element.43.k_ref.v_ref, ...), custom_call_target="tpu_custom_call", output_to_operand_aliasing={{}: (6, {})} | custom-call | flops 6442450944 | bytes 18874368 | tf_op jit(solution)/shard_map/attend_half/pallas_call | solution.py:244
  212.3 28.5 %out_project.3 = (bf16[1536,2048]{1,0:T(8,128)(2,1)}, bf16[1536,2048]{1,0:T(8,128)(2,1)}) custom-call(bf16[1536,3072]{1,0:T(8,128)(2,1)} %bitcast.37, bf16[1536,2048]{1,0:T(8,128)(2,1)} %bitcast.35, bf16[3,3072,2048]{2,1,0:T(8,128)(2,1)} %bitcast.47, f32[1,2048]{1,0:T(1,128)} %get-tuple-element.62.g_ref), custom_call_target="tpu_custom_call" | custom-call | flops 19327352832 | bytes 12582912 | tf_op jit(solution)/shard_map/out_project/pallas_call | solution.py:299
  240.8 123.4 %mlp.5 = (bf16[8,192,2048]{2,1,0:T(8,128)(2,1)}, bf16[8,192,2048]{2,1,0:T(8,128)(2,1)}) custom-call(bf16[8,192,2048]{2,1,0:T(8,128)(2,1)} %bitcast.55, bf16[8,192,2048]{2,1,0:T(8,128)(2,1)} %bitcast.54, bf16[3,2048,8192]{2,1,0:T(8,128)(2,1)} %up_ref.9, bf16[3,8192,2048]{2,1,0:T(8,128)(2,1)} %down_ref.9, f32[1,2048]{1,0:T(1,128)} %get-tuple-element.66.refs_0_), custom_call_target="tpu_custom_call" | custom-call | flops 103079215104 | bytes 67108864 | tf_op jit(solution)/shard_map/mlp/pallas_call | solution.py:370
  364.2 72.5 %qkv_later.2 = (bf16[8,192,9216]{2,1,0:T(8,128)(2,1)}, bf16[8,64,6144]{2,1,0:T(8,128)(2,1)}) custom-call(bf16[8,192,2048]{2,1,0:T(8,128)(2,1)} %get-tuple-element.47.x_ref, bf16[3,2048,24,128]{3,2,1,0:T(8,128)(2,1)} %wq_ref.9, bf16[3,2048,24,128]{3,2,1,0:T(8,128)(2,1)} %wk_ref.9, bf16[3,2048,24,128]{3,2,1,0:T(8,128)(2,1)} %wv_ref.9, ...), custom_call_target="tpu_custom_call" | custom-call | flops 57982058496 | bytes 37748736 | tf_op jit(solution)/shard_map/qkv_later/pallas_call | solution.py:125
  437.2 26.8 %attend_whole.4.prev_ref = bf16[8,192,3072]{2,1,0:T(8,128)(2,1)} custom-call(bf16[8,192,9216]{2,1,0:T(8,128)(2,1)} %get-tuple-element.48.q_ref.k_ref.v_ref, bf16[8,192,9216]{2,1,0:T(8,128)(2,1)} %get-tuple-element.48.q_ref.k_ref.v_ref, bf16[8,192,9216]{2,1,0:T(8,128)(2,1)} %get-tuple-element.48.q_ref.k_ref.v_ref), custom_call_target="tpu_custom_call" | custom-call | flops 25769803776 | bytes 25165824 | tf_op jit(solution)/shard_map/attend_whole/pallas_call | solution.py:230
  464.0 19.4 %attend_half.4 = bf16[8,192,3072]{2,1,0:T(8,128)(2,1)} custom-call(s32[1]{0:T(128)} %bitcast.core_ref, bf16[8,192,9216]{2,1,0:T(8,128)(2,1)} %get-tuple-element.48.q_ref.k_ref.v_ref, bf16[8,64,6144]{2,1,0:T(8,128)(2,1)} %get-tuple-element.49.k_ref.v_ref, bf16[8,64,6144]{2,1,0:T(8,128)(2,1)} %get-tuple-element.49.k_ref.v_ref, ...), custom_call_target="tpu_custom_call", output_to_operand_aliasing={{}: (6, {})} | custom-call | flops 6442450944 | bytes 18874368 | tf_op jit(solution)/shard_map/attend_half/pallas_call | solution.py:244
  483.4 28.5 %out_project.4 = (bf16[1536,2048]{1,0:T(8,128)(2,1)}, bf16[1536,2048]{1,0:T(8,128)(2,1)}) custom-call(bf16[1536,3072]{1,0:T(8,128)(2,1)} %bitcast.38, bf16[1536,2048]{1,0:T(8,128)(2,1)} %bitcast.51, bf16[3,3072,2048]{2,1,0:T(8,128)(2,1)} %bitcast.48, f32[1,2048]{1,0:T(1,128)} %get-tuple-element.63.g_ref), custom_call_target="tpu_custom_call" | custom-call | flops 19327352832 | bytes 12582912 | tf_op jit(solution)/shard_map/out_project/pallas_call | solution.py:299
  511.9 123.2 %mlp.6 = (bf16[8,192,2048]{2,1,0:T(8,128)(2,1)}, bf16[8,192,2048]{2,1,0:T(8,128)(2,1)}) custom-call(bf16[8,192,2048]{2,1,0:T(8,128)(2,1)} %bitcast.53, bf16[8,192,2048]{2,1,0:T(8,128)(2,1)} %bitcast.52, bf16[3,2048,8192]{2,1,0:T(8,128)(2,1)} %up_ref.9, bf16[3,8192,2048]{2,1,0:T(8,128)(2,1)} %down_ref.9, f32[1,2048]{1,0:T(1,128)} %get-tuple-element.64.refs_0_), custom_call_target="tpu_custom_call" | custom-call | flops 103079215104 | bytes 67108864 | tf_op jit(solution)/shard_map/mlp/pallas_call | solution.py:370
  635.1 72.4 %qkv_later.3 = (bf16[8,192,9216]{2,1,0:T(8,128)(2,1)}, bf16[8,64,6144]{2,1,0:T(8,128)(2,1)}) custom-call(bf16[8,192,2048]{2,1,0:T(8,128)(2,1)} %get-tuple-element.53.x_ref, bf16[3,2048,24,128]{3,2,1,0:T(8,128)(2,1)} %wq_ref.9, bf16[3,2048,24,128]{3,2,1,0:T(8,128)(2,1)} %wk_ref.9, bf16[3,2048,24,128]{3,2,1,0:T(8,128)(2,1)} %wv_ref.9, ...), custom_call_target="tpu_custom_call" | custom-call | flops 57982058496 | bytes 37748736 | tf_op jit(solution)/shard_map/qkv_later/pallas_call | solution.py:125
  707.6 26.8 %attend_whole.5.prev_ref = bf16[8,192,3072]{2,1,0:T(8,128)(2,1)} custom-call(bf16[8,192,9216]{2,1,0:T(8,128)(2,1)} %get-tuple-element.54.q_ref.k_ref.v_ref, bf16[8,192,9216]{2,1,0:T(8,128)(2,1)} %get-tuple-element.54.q_ref.k_ref.v_ref, bf16[8,192,9216]{2,1,0:T(8,128)(2,1)} %get-tuple-element.54.q_ref.k_ref.v_ref), custom_call_target="tpu_custom_call" | custom-call | flops 25769803776 | bytes 25165824 | tf_op jit(solution)/shard_map/attend_whole/pallas_call | solution.py:230
  734.4 19.4 %attend_half.5 = bf16[8,192,3072]{2,1,0:T(8,128)(2,1)} custom-call(s32[1]{0:T(128)} %bitcast.core_ref, bf16[8,192,9216]{2,1,0:T(8,128)(2,1)} %get-tuple-element.54.q_ref.k_ref.v_ref, bf16[8,64,6144]{2,1,0:T(8,128)(2,1)} %get-tuple-element.55.k_ref.v_ref, bf16[8,64,6144]{2,1,0:T(8,128)(2,1)} %get-tuple-element.55.k_ref.v_ref, ...), custom_call_target="tpu_custom_call", output_to_operand_aliasing={{}: (6, {})} | custom-call | flops 6442450944 | bytes 18874368 | tf_op jit(solution)/shard_map/attend_half/pallas_call | solution.py:244
  753.8 28.5 %out_project.5 = (bf16[1536,2048]{1,0:T(8,128)(2,1)}, bf16[1536,2048]{1,0:T(8,128)(2,1)}) custom-call(bf16[1536,3072]{1,0:T(8,128)(2,1)} %bitcast.36, bf16[1536,2048]{1,0:T(8,128)(2,1)} %bitcast.50, bf16[3,3072,2048]{2,1,0:T(8,128)(2,1)} %bitcast.49, f32[1,2048]{1,0:T(1,128)} %get-tuple-element.61.g_ref), custom_call_target="tpu_custom_call" | custom-call | flops 19327352832 | bytes 12582912 | tf_op jit(solution)/shard_map/out_project/pallas_call | solution.py:299
  782.3 45.6 %mlp.9 = bf16[8,64,2048]{2,1,0:T(8,128)(2,1)} custom-call(bf16[8,192,2048]{2,1,0:T(8,128)(2,1)} %bitcast.32, bf16[8,192,2048]{2,1,0:T(8,128)(2,1)} %bitcast.29, bf16[3,2048,8192]{2,1,0:T(8,128)(2,1)} %up_ref.9, bf16[3,8192,2048]{2,1,0:T(8,128)(2,1)} %down_ref.9), custom_call_target="tpu_custom_call" | custom-call | flops 34359738368 | bytes 67108864 | tf_op jit(solution)/shard_map/mlp/pallas_call | solution.py:370
  827.9 5.3 all-to-all-start.5
  833.3 45.5 %mlp.8 = bf16[8,64,2048]{2,1,0:T(8,128)(2,1)} custom-call(bf16[8,192,2048]{2,1,0:T(8,128)(2,1)} %bitcast.33, bf16[8,192,2048]{2,1,0:T(8,128)(2,1)} %bitcast.30, bf16[3,2048,8192]{2,1,0:T(8,128)(2,1)} %up_ref.9, bf16[3,8192,2048]{2,1,0:T(8,128)(2,1)} %down_ref.9), custom_call_target="tpu_custom_call" | custom-call | flops 34359738368 | bytes 67108864 | tf_op jit(solution)/shard_map/mlp/pallas_call | solution.py:370
  883.9 45.4 %mlp.7 = bf16[8,64,2048]{2,1,0:T(8,128)(2,1)} custom-call(bf16[8,192,2048]{2,1,0:T(8,128)(2,1)} %bitcast.34, bf16[8,192,2048]{2,1,0:T(8,128)(2,1)} %bitcast.31, bf16[3,2048,8192]{2,1,0:T(8,128)(2,1)} %up_ref.9, bf16[3,8192,2048]{2,1,0:T(8,128)(2,1)} %down_ref.9), custom_call_target="tpu_custom_call" | custom-call | flops 34359738368 | bytes 67108864 | tf_op jit(solution)/shard_map/mlp/pallas_call | solution.py:370
  929.3 31.9 %all_to_all.30 = bf16[8,64,2048]{2,1,0:T(8,128)(2,1)S(1)} all-to-all(bf16[8,64,2048]{2,1,0:T(8,128)(2,1)} %mlp.7), channel_id=1, replica_groups=mesh['data'=2,'seq'=8] {'seq'}, dimensions={0} | all-to-all | bytes 4194304 | tf_op jit(solution)/shard_map/all_to_all | solution.py:405
  961.2 6.0 pad_maximum_fusion
  (28 shorter events, 34.0 us)
Async XLA Ops:
  0.0 34.9 %copy-start = (f32[3,2048]{1,0:T(4,128)S(1)}, f32[3,2048]{1,0:T(4,128)}, u32[]{:S(2)}) copy-start(f32[3,2048]{1,0:T(4,128)} %param.18) | copy-start | bytes 73732
  27.4 31.5 %all-to-all-start = ((bf16[8,64,2048]{2,1,0:T(8,128)(2,1)}), bf16[8,64,2048]{2,1,0:T(8,128)(2,1)}, u32[]{:S(2)}, u32[]{:S(2)}) async-start(bf16[8,64,2048]{2,1,0:T(8,128)(2,1)} %bitcast.2), calls=%async_computation | async-start | bytes 4194304 | tf_op jit(solution)/shard_map/all_to_all | solution.py:405
  58.9 38.9 %all-to-all-start.1 = ((bf16[8,64,2048]{2,1,0:T(8,128)(2,1)}), bf16[8,64,2048]{2,1,0:T(8,128)(2,1)}, u32[]{:S(2)}, u32[]{:S(2)}) async-start(bf16[8,64,2048]{2,1,0:T(8,128)(2,1)} %bitcast.5), calls=%async_computation.1 | async-start | bytes 4194304 | tf_op jit(solution)/shard_map/all_to_all | solution.py:405
  65.1 37.9 %copy-start.1 = (f32[3,2048]{1,0:T(4,128)S(1)}, f32[3,2048]{1,0:T(4,128)}, u32[]{:S(2)}) copy-start(f32[3,2048]{1,0:T(4,128)} %param.19) | copy-start | bytes 73732
  97.7 95.3 %collective-permute-start = (bf16[8,64,6144]{2,1,0:T(8,128)(2,1)}, bf16[8,64,6144]{2,1,0:T(8,128)(2,1)}, u32[]{:S(2)}, u32[]{:S(2)}) collective-permute-start(bf16[8,64,6144]{2,1,0:T(8,128)(2,1)} %get-tuple-element.43.k_ref.v_ref), channel_id=1, source_target_pairs={{0,1},{1,0},{2,3},{3,2},{4,5},{5,4},{6,7},{7,6},{8,9},{9,8},{10,11... | collective-permute-start | bytes 18874376 | tf_op jit(solution)/shard_map/ppermute | solution.py:434
  97.9 36.9 %all-to-all-start.2 = ((bf16[8,64,2048]{2,1,0:T(8,128)(2,1)}), bf16[8,64,2048]{2,1,0:T(8,128)(2,1)}, u32[]{:S(2)}, u32[]{:S(2)}) async-start(bf16[8,64,2048]{2,1,0:T(8,128)(2,1)} %bitcast.39), calls=%async_computation.2 | async-start | bytes 4194304 | tf_op jit(solution)/shard_map/all_to_all | solution.py:405
  436.7 27.3 %collective-permute-start.1 = (bf16[8,64,6144]{2,1,0:T(8,128)(2,1)}, bf16[8,64,6144]{2,1,0:T(8,128)(2,1)}, u32[]{:S(2)}, u32[]{:S(2)}) collective-permute-start(bf16[8,64,6144]{2,1,0:T(8,128)(2,1)} %get-tuple-element.49.k_ref.v_ref), channel_id=1, source_target_pairs={{0,1},{1,0},{2,3},{3,2},{4,5},{5,4},{6,7},{7,6},{8,9},{9,8},{10,11... | collective-permute-start | bytes 18874376 | tf_op jit(solution)/shard_map/ppermute | solution.py:434
  707.5 26.9 %collective-permute-start.2 = (bf16[8,64,6144]{2,1,0:T(8,128)(2,1)}, bf16[8,64,6144]{2,1,0:T(8,128)(2,1)}, u32[]{:S(2)}, u32[]{:S(2)}) collective-permute-start(bf16[8,64,6144]{2,1,0:T(8,128)(2,1)} %get-tuple-element.55.k_ref.v_ref), channel_id=1, source_target_pairs={{0,1},{1,0},{2,3},{3,2},{4,5},{5,4},{6,7},{7,6},{8,9},{9,8},{10,11... | collective-permute-start | bytes 18874376 | tf_op jit(solution)/shard_map/ppermute | solution.py:434
  827.9 50.8 %all-to-all-start.5 = ((bf16[8,64,2048]{2,1,0:T(8,128)(2,1)}), bf16[8,64,2048]{2,1,0:T(8,128)(2,1)}, u32[]{:S(2)}, u32[]{:S(2)}) async-start(bf16[8,64,2048]{2,1,0:T(8,128)(2,1)} %mlp.9), calls=%async_computation.5 | async-start | bytes 4194304 | tf_op jit(solution)/shard_map/all_to_all | solution.py:405
  878.7 50.6 %all-to-all-start.4 = ((bf16[8,64,2048]{2,1,0:T(8,128)(2,1)}), bf16[8,64,2048]{2,1,0:T(8,128)(2,1)}, u32[]{:S(2)}, u32[]{:S(2)}) async-start(bf16[8,64,2048]{2,1,0:T(8,128)(2,1)} %mlp.8), calls=%async_computation.4 | async-start | bytes 4194304 | tf_op jit(solution)/shard_map/all_to_all | solution.py:405

commit v3 on v2

--- a/solution.py
+++ b/solution.py
@@ -6,6 +6,7 @@
 from jax.experimental import pallas as pl
 from jax.experimental.pallas import tpu as pltpu
 from jax.sharding import PartitionSpec as P
+
 
 ROPE_BASE = 10000.0
 NORM_EPS = 1e-6
@@ -116,7 +117,7 @@
 
 
 def qkv_later(x, w_query, w_key, w_value, cos, sin, layer, piece):
-    shards, per_shard, depth = x.shape
+    shards, per_shard, _ = x.shape
     heads, dh = w_query.shape[2:]
     hb = 8
     w_specs, steps = weight_specs(w_query, layer, hb)
@@ -239,6 +240,7 @@
         ),
         name="attend_whole",
     )(qkv, qkv, qkv)
+    width, steps = 2 * width, steps // 2
     shared = pl.BlockSpec((shards, piece, width), lambda h: (0, 2, h))
     side = lambda second: pl.BlockSpec((shards, piece, width), lambda h: (0, 0, second * steps + h))
     return pl.pallas_call(
@@ -264,128 +266,113 @@
     )(core, qkv, kv_own, kv_own, kv_other, kv_other, out)
 
 
-def out_kernel(sub, o_ref, x_ref, w_ref, g_ref, h_ref, r_ref, acc):
-    k, m = pl.program_id(0), pl.program_id(1)
-    last = pl.num_programs(0) - 1
-    rows = o_ref.shape[0]
-    dot = lambda r: jnp.dot(o_ref[r : r + sub, :], w_ref[...], preferred_element_type=jnp.float32)
-
-    @pl.when(k == 0)
+def tail_kernel(nk, group, o_ref, x_ref, wo_ref, gm_ref, up_ref, down_ref, *refs):
+    if len(refs) == 4:
+        ga_ref, y_ref, r_ref, acc = refs
+    else:
+        ga_ref, (y_ref, r_ref, acc) = None, refs
+    step = pl.program_id(1)
+    groups, per, width = x_ref.shape
+    sub = group * per
+    starts = range(0, groups, group)
+    rows = lambda lo: slice(lo * per, lo * per + sub)
+    project = lambda lo, n: jnp.dot(flat(o_ref, lo, n), wo_ref[...], preferred_element_type=jnp.float32)
+    up = lambda lo: jnp.dot(flat(r_ref, lo, group), up_ref[...], preferred_element_type=jnp.float32)
+
+    def pipelined(issue, finish):
+        held = issue(0)
+        for lo in starts:
+            ahead = issue(lo + group) if lo + group < groups else None
+            finish(lo, held)
+            held = ahead
+
+    @pl.when(step == 0)
     def _():
-        for r in range(0, rows, sub):
-            acc[m, r : r + sub, :] = dot(r)
-
-    @pl.when((k > 0) & (k < last))
+        acc[...] = project(0, groups)
+
+    @pl.when((step > 0) & (step < nk - 1))
     def _():
-        for r in range(0, rows, sub):
-            acc[m, r : r + sub, :] += dot(r)
-
-    @pl.when(k == last)
+        acc[...] += project(0, groups)
+
+    @pl.when(step == nk - 1)
     def _():
-        held = dot(0)
-        for r in range(0, rows, sub):
-            ahead = dot(r + sub) if r + sub < rows else None
-            h = (x_ref[r : r + sub, :].astype(jnp.float32) + (acc[m, r : r + sub, :] + held)).astype(jnp.bfloat16)
-            h_ref[r : r + sub, :] = h
-            r_ref[r : r + sub, :] = norm_rows(h.astype(jnp.float32), g_ref[...])
-            held = ahead
-
-
-def out_project(o, x, w_out, gain, layer):
-    rows, depth = o.shape
-    width = x.shape[1]
-    mb, tk = 512, depth // 2
-    at_end = pl.BlockSpec((mb, width), lambda k, m: (jnp.where(k == depth // tk - 1, m, 0), 0))
-    return pl.pallas_call(
-        functools.partial(out_kernel, 256),
-        grid=(depth // tk, rows // mb),
-        in_specs=[
-            pl.BlockSpec((mb, tk), lambda k, m: (m, k)),
-            at_end,
-            pl.BlockSpec((None, tk, width), lambda k, m: (layer, k, 0)),
-            pl.BlockSpec((1, width), lambda k, m: (0, 0)),
-        ],
-        out_specs=[at_end] * 2,
-        out_shape=[jax.ShapeDtypeStruct((rows, width), jnp.bfloat16)] * 2,
-        scratch_shapes=[pltpu.VMEM((rows // mb, mb, width), jnp.float32)],
-        compiler_params=pltpu.CompilerParams(vmem_limit_bytes=VMEM_LIMIT),
-        cost_estimate=pl.CostEstimate(
-            flops=2 * rows * depth * width, bytes_accessed=2 * depth * width, transcendentals=0
-        ),
-        name="out_project",
-    )(o, x, w_out, gain)
-
-
-def mlp_kernel(group, r_ref, h_ref, up_ref, down_ref, *refs):
-    g_ref, y_ref, n_ref, acc = refs if len(refs) == 4 else (None, refs[0], None, refs[1])
-    f = pl.program_id(1)
-    groups, per, width = r_ref.shape
-    sub = group * per
-    up = lambda lo: jnp.dot(flat(r_ref, lo, group), up_ref[...], preferred_element_type=jnp.float32)
+        def finish(lo, prod):
+            total = acc[rows(lo), :] + prod
+            h = (flat(x_ref, lo, group).astype(jnp.float32) + total).astype(jnp.bfloat16)
+            y_ref[lo : lo + group] = h.reshape(group, per, width)
+            r_ref[lo : lo + group] = norm_rows(h.astype(jnp.float32), gm_ref[...]).reshape(group, per, width)
+
+        pipelined(lambda lo: project(lo, group), finish)
 
     def add_block(first):
-        held = up(0)
-        for lo in range(0, groups, group):
-            ahead = up(lo + group) if lo + group < groups else None
-            z = jax.nn.gelu(held, approximate=True).astype(jnp.bfloat16)
+        def finish(lo, u):
+            z = jax.nn.gelu(u, approximate=True).astype(jnp.bfloat16)
             prod = jnp.dot(z, down_ref[...], preferred_element_type=jnp.float32)
-            rows = slice(lo * per, lo * per + sub)
             if first:
-                acc[rows, :] = prod
+                acc[rows(lo), :] = prod
             else:
-                acc[rows, :] += prod
-            held = ahead
-
-    pl.when(f == 0)(lambda: add_block(True))
-    pl.when(f > 0)(lambda: add_block(False))
-
-    @pl.when(f == pl.num_programs(1) - 1)
+                acc[rows(lo), :] += prod
+
+        pipelined(up, finish)
+
+    pl.when(step == nk)(lambda: add_block(True))
+    pl.when(step > nk)(lambda: add_block(False))
+
+    @pl.when(step == pl.num_programs(1) - 1)
     def _():
         for lo in range(groups):
-            rows = slice(lo * per, (lo + 1) * per)
-            y = (h_ref[lo].astype(jnp.float32) + acc[rows, :]).astype(jnp.bfloat16)
+            y = (y_ref[lo].astype(jnp.float32) + acc[lo * per : (lo + 1) * per, :]).astype(jnp.bfloat16)
             y_ref[lo] = y
-            if n_ref is not None:
-                n_ref[lo] = norm_rows(y.astype(jnp.float32), g_ref[...])
-
-
-def mlp(r, h, w_up, w_down, gain, layer, part=None, piece=None):
-    shards, per_shard, width = r.shape
+            if ga_ref is not None:
+                r_ref[lo] = norm_rows(y.astype(jnp.float32), ga_ref[...])
+
+
+def layer_tail(o, x, w_out, gain_mlp, w_up, w_down, gain_next, layer, part=None):
+    shards, per_shard, width = x.shape
+    depth = o.shape[2]
     ff = w_up.shape[2]
-    tf = 1024
+    tf = tk = 1024
+    nk = depth // tk
+    early = lambda s: jnp.minimum(s, nk - 1)
+    late = lambda s: jnp.maximum(s - nk, 0)
+    gain_spec = pl.BlockSpec((1, width), lambda m, s: (0, 0))
     if part is None:
-        blocks, block = 2, (shards // 2, per_shard, width)
-        group = shards // 4
-        in_row = out_row = pl.BlockSpec(block, lambda m, f: (m, 0, 0))
-        extra, extra_specs = [gain], [pl.BlockSpec((1, width), lambda m, f: (0, 0))]
-        out_shape = [jax.ShapeDtypeStruct(r.shape, jnp.bfloat16)] * 2
+        blocks, block, group = 2, (shards // 2, per_shard), shards // 4
+        place = lambda m: (m, 0)
+        out_row = pl.BlockSpec((*block, width), lambda m, s: (m, 0, 0))
+        extra, extra_specs = [gain_next], [gain_spec]
+        out_shape = [jax.ShapeDtypeStruct(x.shape, jnp.bfloat16)] * 2
+        scratch = []
     else:
-        blocks, block = 1, (shards, piece, width)
-        group = shards // 2
-        in_row = pl.BlockSpec(block, lambda m, f: (0, part, 0))
-        out_row = pl.BlockSpec(block, lambda m, f: (0, 0, 0))
+        blocks, per, run = part
+        block, group = (shards // blocks, per), shards // (2 * blocks)
+        place = lambda m: (m, run)
+        out_row = pl.BlockSpec((*block, width), lambda m, s: (m, 0, 0))
         extra, extra_specs = [], []
-        out_shape = [jax.ShapeDtypeStruct(block, jnp.bfloat16)]
+        out_shape = [jax.ShapeDtypeStruct((shards, per, width), jnp.bfloat16)]
+        scratch = [pltpu.VMEM((*block, width), jnp.bfloat16)]
     rows = blocks * block[0] * block[1]
     return pl.pallas_call(
-        functools.partial(mlp_kernel, group),
-        grid=(blocks, ff // tf),
+        functools.partial(tail_kernel, nk, group),
+        grid=(blocks, nk + ff // tf),
         in_specs=[
-            in_row,
-            in_row,
-            pl.BlockSpec((None, width, tf), lambda m, f: (layer, 0, f)),
-            pl.BlockSpec((None, tf, width), lambda m, f: (layer, f, 0)),
+            pl.BlockSpec((*block, tk), lambda m, s: (*place(m), early(s))),
+            pl.BlockSpec((*block, width), lambda m, s: (*place(m), 0)),
+            pl.BlockSpec((None, tk, width), lambda m, s: (layer, early(s), 0)),
+            gain_spec,
+            pl.BlockSpec((None, width, tf), lambda m, s: (layer, 0, late(s))),
+            pl.BlockSpec((None, tf, width), lambda m, s: (layer, late(s), 0)),
             *extra_specs,
         ],
         out_specs=[out_row] * len(out_shape),
         out_shape=out_shape,
-        scratch_shapes=[pltpu.VMEM((block[0] * block[1], width), jnp.float32)],
+        scratch_shapes=[*scratch, pltpu.VMEM((block[0] * block[1], width), jnp.float32)],
         compiler_params=pltpu.CompilerParams(vmem_limit_bytes=VMEM_LIMIT),
         cost_estimate=pl.CostEstimate(
-            flops=4 * rows * ff * width, bytes_accessed=4 * ff * width, transcendentals=0
+            flops=rows * width * (4 * ff + 2 * depth), bytes_accessed=width * (4 * ff + 2 * depth), transcendentals=0
         ),
-        name="mlp",
-    )(r, h, w_up, w_down, *extra)
+        name="layer_tail",
+    )(o, x, w_out, gain_mlp, w_up, w_down, *extra)
 
 
 def solution(mesh):
@@ -404,15 +391,12 @@
         core = lax.rem(lax.axis_index("seq"), 2)
         exchange = lambda a: lax.all_to_all(a, "seq", 0, 0, tiled=True)
 
-        pos = lax.all_gather(pos_loc, "seq", tiled=True).reshape(n_seq, shard)
+        pos = exchange(jnp.broadcast_to(pos_loc, (n_seq, shard)))
         by_chip = x_loc.reshape(n_pair, per, shard, width)
-        sends = [by_chip[:, :2, i * piece : (i + 1) * piece].reshape(n_seq, piece, width) for i in range(2)]
-        first, pos = lax.optimization_barrier((by_chip[:, 2].reshape(n_seq, piece, width), pos))
-        shared_x = exchange(first)
-        shared_x, send0 = lax.optimization_barrier((shared_x, sends[0]))
-        x0 = exchange(send0)
-        x0, send1 = lax.optimization_barrier((x0, sends[1]))
-        x1 = exchange(send1)
+        pos, send = lax.optimization_barrier((pos, by_chip[:, 2].reshape(n_seq, piece, width)))
+        shared_x = exchange(send)
+        shared_x, send = lax.optimization_barrier((shared_x, by_chip[:, :2].reshape(n_seq, shard, width)))
+        whole_x = exchange(send)
 
         pos_shared = lax.dynamic_index_in_dim(pos.reshape(n_seq, 2, piece), core, axis=1, keepdims=False)
         inv_freq = ROPE_BASE ** (-jnp.arange(dh // 2, dtype=jnp.float32) * (2.0 / dh))
@@ -422,28 +406,26 @@
         sin = jnp.concatenate([-sin, sin], axis=-1)
         core_arr = core.astype(jnp.int32).reshape(1)
         w_out2 = w_out.reshape(n_layers, heads * dh, width)
-        flat2 = lambda a: a.reshape(-1, a.shape[-1])
 
         first_args = (w_query, w_key, w_value, cos, sin, g_attn[0][None])
         qkv, hidden, kv_own = qkv_first(shared_x, 2, [], *first_args, True)
-        qkv, hidden = qkv_first(x0, 0, [qkv, hidden], *first_args, False)
-        qkv, hidden = qkv_first(x1, 1, [qkv, hidden], *first_args, False)
+        qkv, hidden = qkv_first(whole_x, 0, [qkv, hidden], *first_args, False)
         for layer in range(n_layers):
             if layer:
                 qkv, kv_own = qkv_later(normed, w_query, w_key, w_value, cos, sin, layer, piece)
             kv_other = lax.ppermute(kv_own, "seq", partner)
             attn = attention(qkv, kv_own, kv_other, core_arr, heads, dh)
-            resid, r = out_project(flat2(attn), flat2(hidden), w_out2, g_mlp[layer][None], layer)
-            resid, r = resid.reshape(hidden.shape), r.reshape(hidden.shape)
+            tail_args = (attn, hidden, w_out2, g_mlp[layer][None], w_up, w_down)
             if layer < n_layers - 1:
-                hidden, normed = mlp(r, resid, w_up, w_down, g_attn[layer + 1][None], layer)
-
-        parts = []
-        for part in range(3):
-            (y,) = mlp(r, resid, w_up, w_down, None, n_layers - 1, part, piece)
-            parts.append(exchange(y))
-        whole = jnp.concatenate([a.reshape(n_pair, 2, piece, width) for a in parts[:2]], axis=2)
-        shared = parts[2].reshape(n_pair, 1, shard, width)
+                hidden, normed = layer_tail(*tail_args, g_attn[layer + 1][None], layer)
+
+        (y_whole,) = layer_tail(*tail_args, None, n_layers - 1, (2, shard, 0))
+        y_whole = exchange(y_whole)
+        (y_shared,) = layer_tail(*tail_args, None, n_layers - 1, (1, piece, 2))
+        y_whole, y_shared = lax.optimization_barrier((y_whole, y_shared))
+        y_shared = exchange(y_shared)
+        whole = y_whole.reshape(n_pair, 2, shard, width)
+        shared = y_shared.reshape(n_pair, 1, shard, width)
         return jnp.concatenate([whole, shared], axis=1).reshape(n_batch, shard, width)
 
     return jax.shard_map(device_fn, mesh=mesh, in_specs=in_specs, out_specs=tok_spec, check_vma=False)

time: 977 us -> 950 us (0.972)
  blocking collectives: 56.1 us -> 31.8 us
  waiting for transfers between devices: 18.6 us -> 35.1 us
  Pallas kernels: 847 us -> 834 us
    all_gather x1 -> x0, blocking collectives: 24.2 us -> none  [device_fn(): pos = lax.all_gather(pos_loc, 'seq', tiled=True).reshape(n_seq, shard)]
    all_to_all x5 -> x4, waiting for transfers between devices: 18.6 us -> 35.1 us  [device_fn(): exchange = lambda a: lax.all_to_all(a, 'seq', 0, 0, tiled=True)]
    pallas_call x8 -> x4, Pallas kernels: 469 us -> 458 us  [layer_tail(): pl.pallas_call(functools.partial(tail_kernel, nk, group), grid=(blocks, n...]
    all_to_all x5 -> x4, starting transfers between devices: 24.7 us -> 18.6 us  [device_fn(): exchange = lambda a: lax.all_to_all(a, 'seq', 0, 0, tiled=True)]
    pallas_call x3 -> x2, Pallas kernels: 95 us -> 97.6 us  [qkv_first(): pl.pallas_call(functools.partial(first_kernel, steps, with_kv, len(prev))...]
  transfers between devices with their start and end apart: 8 -> 7, of which waited for: 1 -> 3; matrix products, arithmetic and copies ran while one was open for 1% -> 1% of each run, Pallas kernels for 28% -> 25%
where the time goes in v3:
time: 950 us; the launch traced here: 941 us
  Pallas kernels  834 us (88%)
  waiting for transfers between devices  35.1 us (4%)
  blocking collectives  31.8 us (3%)
  starting transfers between devices  19.4 us (2%)
  local copies, waits for them, and re-layouts  10.5 us (1%)
  other arithmetic  9.87 us (1%)
    pallas_call x4, Pallas kernels, layer_tail(): pl.pallas_call(functools.partial(tail_kernel, nk, group), grid=(blocks, n...  458 us
    pallas_call x2, Pallas kernels, qkv_later(): pl.pallas_call(functools.partial(later_kernel, steps, shards // 2, per_sh...  144 us
    pallas_call x2, Pallas kernels, qkv_first(): pl.pallas_call(functools.partial(first_kernel, steps, with_kv, len(prev))...  97.6 us
    pallas_call x3, Pallas kernels, attention(): pl.pallas_call(functools.partial(whole_kernel, tile, scale2, dh), grid=(s...  80.2 us
    pallas_call x3, Pallas kernels, attention(): pl.pallas_call(functools.partial(half_kernel, tile, scale2, dh), grid=(st...  54.4 us
    all_to_all x4, waiting for transfers between devices, device_fn(): exchange = lambda a: lax.all_to_all(a, 'seq', 0, 0, tiled=True)  35.1 us
    all_to_all x1, blocking collectives, device_fn(): exchange = lambda a: lax.all_to_all(a, 'seq', 0, 0, tiled=True)  31.8 us
  transfers between devices with their start and end apart: 7, of which 3 were waited for; matrix products, arithmetic and copies ran while one was open for 1% of the time, Pallas kernels for 25%

profile of v3, /device:TPU:112, one launch (start us, length us, event | category | flops | bytes accessed | tf_op | source)
XLA Modules:
  0.0 941.3 jit_solution(1261034655810679396)
XLA Ops:
  1.2 5.3 all-to-all-start
  6.5 3.2 slice.32
  11.8 3.8 all-to-all-start.1
  15.7 4.7 slice.33
  20.4 22.2 %all-to-all-done.1.x_ref = bf16[8,64,2048]{2,1,0:T(8,128)(2,1)S(1)} async-done(((bf16[8,64,2048]{2,1,0:T(8,128)(2,1)}), bf16[8,64,2048]{2,1,0:T(8,128)(2,1)S(1)}, u32[]{:S(2)}, u32[]{:S(2)}) %all-to-all-start.1) | async-done | bytes 2097184 | tf_op jit(solution)/shard_map/all_to_all | solution.py:392
  42.6 4.7 all-to-all-start.2
  52.5 32.8 %qkv_first.2 = (bf16[8,192,9216]{2,1,0:T(8,128)(2,1)}, bf16[8,192,2048]{2,1,0:T(8,128)(2,1)}, bf16[8,64,6144]{2,1,0:T(8,128)(2,1)}) custom-call(bf16[8,64,2048]{2,1,0:T(8,128)(2,1)} %copy-done, f32[1,2048]{1,0:T(1,128)} %get-tuple-element.47.g_ref, bf16[3,2048,24,128]{3,2,1,0:T(8,128)(2,1)} %wq_ref.7, bf16[3,2048,24,128]{3,2,1,0:T(8,128)(2,1)} %wk_ref.7, ...), custom_call_target="tpu_custom_call" | custom-call | flops 19327352832 | bytes 37748736 | tf_op jit(solution)/shard_map/qkv_first/pallas_call | solution.py:104
  86.1 10.7 %all-to-all-done.2.x_ref = bf16[8,128,2048]{2,1,0:T(8,128)(2,1)} async-done(((bf16[8,128,2048]{2,1,0:T(8,128)(2,1)}), bf16[8,128,2048]{2,1,0:T(8,128)(2,1)}, u32[]{:S(2)}, u32[]{:S(2)}) %all-to-all-start.2) | async-done | bytes 4194336 | tf_op jit(solution)/shard_map/all_to_all | solution.py:392
  96.9 64.8 %qkv_first.3 = (bf16[8,192,9216]{2,1,0:T(8,128)(2,1)}, bf16[8,192,2048]{2,1,0:T(8,128)(2,1)}) custom-call(bf16[8,128,2048]{2,1,0:T(8,128)(2,1)} %all-to-all-done.2.x_ref, f32[1,2048]{1,0:T(1,128)} %get-tuple-element.47.g_ref, bf16[3,2048,24,128]{3,2,1,0:T(8,128)(2,1)} %wq_ref.7, ...), custom_call_target="tpu_custom_call", output_to_operand_aliasing={{0}: (7, {}), {1}: (8, {})} | custom-call | flops 38654705664 | bytes 37748736 | tf_op jit(solution)/shard_map/qkv_first/pallas_call | solution.py:104
  161.7 26.8 %attend_whole.3.prev_ref = bf16[8,192,3072]{2,1,0:T(8,128)(2,1)} custom-call(bf16[8,192,9216]{2,1,0:T(8,128)(2,1)} %get-tuple-element.30.q_ref.k_ref.v_ref, bf16[8,192,9216]{2,1,0:T(8,128)(2,1)} %get-tuple-element.30.q_ref.k_ref.v_ref, bf16[8,192,9216]{2,1,0:T(8,128)(2,1)} %get-tuple-element.30.q_ref.k_ref.v_ref), custom_call_target="tpu_custom_call" | custom-call | flops 25769803776 | bytes 25165824 | tf_op jit(solution)/shard_map/attend_whole/pallas_call | solution.py:231
  188.4 18.1 %attend_half.3.o_ref = bf16[8,192,3072]{2,1,0:T(8,128)(2,1)} custom-call(s32[1]{0:T(128)} %bitcast.core_ref, bf16[8,192,9216]{2,1,0:T(8,128)(2,1)} %get-tuple-element.30.q_ref.k_ref.v_ref, bf16[8,64,6144]{2,1,0:T(8,128)(2,1)} %get-tuple-element.31.k_ref.v_ref, bf16[8,64,6144]{2,1,0:T(8,128)(2,1)} %get-tuple-element.31.k_ref.v_ref, ...), custom_call_target="tpu_custom_call", output_to_operand_aliasing={{}: (6, {})} | custom-call | flops 6442450944 | bytes 18874368 | tf_op jit(solution)/shard_map/attend_half/pallas_call | solution.py:246
  206.6 149.4 %layer_tail.4 = (bf16[8,192,2048]{2,1,0:T(8,128)(2,1)}, bf16[8,192,2048]{2,1,0:T(8,128)(2,1)}) custom-call(bf16[8,192,3072]{2,1,0:T(8,128)(2,1)} %attend_half.3.o_ref, bf16[8,192,2048]{2,1,0:T(8,128)(2,1)} %get-tuple-element.32.x_ref, bf16[3,3072,2048]{2,1,0:T(8,128)(2,1)} %bitcast.14, f32[1,2048]{1,0:T(1,128)} %get-tuple-element.44.gm_ref, ...), custom_call_target="tpu_custom_call" | custom-call | flops 122406567936 | bytes 79691776 | tf_op jit(solution)/shard_map/layer_tail/pallas_call | solution.py:355
  356.0 72.2 %qkv_later.2 = (bf16[8,192,9216]{2,1,0:T(8,128)(2,1)}, bf16[8,64,6144]{2,1,0:T(8,128)(2,1)}) custom-call(bf16[8,192,2048]{2,1,0:T(8,128)(2,1)} %get-tuple-element.33.x_ref, bf16[3,2048,24,128]{3,2,1,0:T(8,128)(2,1)} %wq_ref.7, bf16[3,2048,24,128]{3,2,1,0:T(8,128)(2,1)} %wk_ref.7, bf16[3,2048,24,128]{3,2,1,0:T(8,128)(2,1)} %wv_ref.7, ...), custom_call_target="tpu_custom_call" | custom-call | flops 57982058496 | bytes 37748736 | tf_op jit(solution)/shard_map/qkv_later/pallas_call | solution.py:126
  428.3 26.8 %attend_whole.4.prev_ref = bf16[8,192,3072]{2,1,0:T(8,128)(2,1)} custom-call(bf16[8,192,9216]{2,1,0:T(8,128)(2,1)} %get-tuple-element.34.q_ref.k_ref.v_ref, bf16[8,192,9216]{2,1,0:T(8,128)(2,1)} %get-tuple-element.34.q_ref.k_ref.v_ref, bf16[8,192,9216]{2,1,0:T(8,128)(2,1)} %get-tuple-element.34.q_ref.k_ref.v_ref), custom_call_target="tpu_custom_call" | custom-call | flops 25769803776 | bytes 25165824 | tf_op jit(solution)/shard_map/attend_whole/pallas_call | solution.py:231
  455.1 18.1 %attend_half.4.o_ref = bf16[8,192,3072]{2,1,0:T(8,128)(2,1)} custom-call(s32[1]{0:T(128)} %bitcast.core_ref, bf16[8,192,9216]{2,1,0:T(8,128)(2,1)} %get-tuple-element.34.q_ref.k_ref.v_ref, bf16[8,64,6144]{2,1,0:T(8,128)(2,1)} %get-tuple-element.35.k_ref.v_ref, bf16[8,64,6144]{2,1,0:T(8,128)(2,1)} %get-tuple-element.35.k_ref.v_ref, ...), custom_call_target="tpu_custom_call", output_to_operand_aliasing={{}: (6, {})} | custom-call | flops 6442450944 | bytes 18874368 | tf_op jit(solution)/shard_map/attend_half/pallas_call | solution.py:246
  473.2 149.5 %layer_tail.5 = (bf16[8,192,2048]{2,1,0:T(8,128)(2,1)}, bf16[8,192,2048]{2,1,0:T(8,128)(2,1)}) custom-call(bf16[8,192,3072]{2,1,0:T(8,128)(2,1)} %attend_half.4.o_ref, bf16[8,192,2048]{2,1,0:T(8,128)(2,1)} %get-tuple-element.36.x_ref, bf16[3,3072,2048]{2,1,0:T(8,128)(2,1)} %bitcast.15, f32[1,2048]{1,0:T(1,128)} %get-tuple-element.45.gm_ref, ...), custom_call_target="tpu_custom_call" | custom-call | flops 122406567936 | bytes 79691776 | tf_op jit(solution)/shard_map/layer_tail/pallas_call | solution.py:355
  622.8 72.0 %qkv_later.3 = (bf16[8,192,9216]{2,1,0:T(8,128)(2,1)}, bf16[8,64,6144]{2,1,0:T(8,128)(2,1)}) custom-call(bf16[8,192,2048]{2,1,0:T(8,128)(2,1)} %get-tuple-element.37.x_ref, bf16[3,2048,24,128]{3,2,1,0:T(8,128)(2,1)} %wq_ref.7, bf16[3,2048,24,128]{3,2,1,0:T(8,128)(2,1)} %wk_ref.7, bf16[3,2048,24,128]{3,2,1,0:T(8,128)(2,1)} %wv_ref.7, ...), custom_call_target="tpu_custom_call" | custom-call | flops 57982058496 | bytes 37748736 | tf_op jit(solution)/shard_map/qkv_later/pallas_call | solution.py:126
  695.3 26.7 %attend_whole.5.prev_ref = bf16[8,192,3072]{2,1,0:T(8,128)(2,1)} custom-call(bf16[8,192,9216]{2,1,0:T(8,128)(2,1)} %get-tuple-element.38.q_ref.k_ref.v_ref, bf16[8,192,9216]{2,1,0:T(8,128)(2,1)} %get-tuple-element.38.q_ref.k_ref.v_ref, bf16[8,192,9216]{2,1,0:T(8,128)(2,1)} %get-tuple-element.38.q_ref.k_ref.v_ref), custom_call_target="tpu_custom_call" | custom-call | flops 25769803776 | bytes 25165824 | tf_op jit(solution)/shard_map/attend_whole/pallas_call | solution.py:231
  722.1 18.1 %attend_half.5.o_ref = bf16[8,192,3072]{2,1,0:T(8,128)(2,1)} custom-call(s32[1]{0:T(128)} %bitcast.core_ref, bf16[8,192,9216]{2,1,0:T(8,128)(2,1)} %get-tuple-element.38.q_ref.k_ref.v_ref, bf16[8,64,6144]{2,1,0:T(8,128)(2,1)} %get-tuple-element.39.k_ref.v_ref, bf16[8,64,6144]{2,1,0:T(8,128)(2,1)} %get-tuple-element.39.k_ref.v_ref, ...), custom_call_target="tpu_custom_call", output_to_operand_aliasing={{}: (6, {})} | custom-call | flops 6442450944 | bytes 18874368 | tf_op jit(solution)/shard_map/attend_half/pallas_call | solution.py:246
  740.2 104.1 %layer_tail.6 = bf16[8,128,2048]{2,1,0:T(8,128)(2,1)} custom-call(bf16[8,192,3072]{2,1,0:T(8,128)(2,1)} %attend_half.5.o_ref, bf16[8,192,2048]{2,1,0:T(8,128)(2,1)} %get-tuple-element.40.x_ref, bf16[3,3072,2048]{2,1,0:T(8,128)(2,1)} %bitcast.16, f32[1,2048]{1,0:T(1,128)} %get-tuple-element.43.gm_ref, bf16[3,2048,8192]{2,1,0:T(8,128)(2,1)} %up_ref.7, ...), custom_call_target="tpu_custom_call" | custom-call | flops 81604378624 | bytes 79691776 | tf_op jit(solution)/shard_map/layer_tail/pallas_call | solution.py:355
  844.3 4.8 all-to-all-start.3
  849.0 54.7 %layer_tail.7 = bf16[8,64,2048]{2,1,0:T(8,128)(2,1)} custom-call(bf16[8,192,3072]{2,1,0:T(8,128)(2,1)} %attend_half.5.o_ref, bf16[8,192,2048]{2,1,0:T(8,128)(2,1)} %get-tuple-element.40.x_ref, bf16[3,3072,2048]{2,1,0:T(8,128)(2,1)} %bitcast.17, f32[1,2048]{1,0:T(1,128)} %get-tuple-element.43.gm_ref, bf16[3,2048,8192]{2,1,0:T(8,128)(2,1)} %up_ref.7, ...), custom_call_target="tpu_custom_call" | custom-call | flops 40802189312 | bytes 79691776 | tf_op jit(solution)/shard_map/layer_tail/pallas_call | solution.py:355
  903.7 31.8 %all_to_all.29 = bf16[8,64,2048]{2,1,0:T(8,128)(2,1)S(1)} all-to-all(bf16[8,64,2048]{2,1,0:T(8,128)(2,1)} %layer_tail.7), channel_id=1, replica_groups=mesh['data'=2,'seq'=8] {'seq'}, dimensions={0} | all-to-all | bytes 4194304 | tf_op jit(solution)/shard_map/all_to_all | solution.py:392
  935.5 5.4 pad_maximum_fusion
  (23 shorter events, 9.9 us)
Async XLA Ops:
  1.2 10.6 %all-to-all-start = ((s32[8,1,128]{2,1,0:T(1,128)}), s32[8,1,128]{2,1,0:T(1,128)S(1)}, u32[]{:S(2)}, u32[]{:S(2)}) async-start(s32[8,1,128]{2,1,0:T(1,128)} %broadcast_in_dim.2), calls=%async_computation | async-start | bytes 8192 | tf_op jit(solution)/shard_map/all_to_all | solution.py:392
  11.8 30.8 %all-to-all-start.1 = ((bf16[8,64,2048]{2,1,0:T(8,128)(2,1)}), bf16[8,64,2048]{2,1,0:T(8,128)(2,1)S(1)}, u32[]{:S(2)}, u32[]{:S(2)}) async-start(bf16[8,64,2048]{2,1,0:T(8,128)(2,1)} %bitcast.3), calls=%async_computation.1 | async-start | bytes 4194304 | tf_op jit(solution)/shard_map/all_to_all | solution.py:392
  20.4 27.0 %copy-start.1 = (f32[3,2048]{1,0:T(4,128)S(1)}, f32[3,2048]{1,0:T(4,128)}, u32[]{:S(2)}) copy-start(f32[3,2048]{1,0:T(4,128)} %param.18) | copy-start | bytes 73732
  42.6 9.9 %copy-start = (bf16[8,64,2048]{2,1,0:T(8,128)(2,1)}, bf16[8,64,2048]{2,1,0:T(8,128)(2,1)S(1)}, u32[]{:S(2)}) copy-start(bf16[8,64,2048]{2,1,0:T(8,128)(2,1)S(1)} %all-to-all-done.1.x_ref) | copy-start | bytes 6291460
  42.6 54.2 %all-to-all-start.2 = ((bf16[8,128,2048]{2,1,0:T(8,128)(2,1)}), bf16[8,128,2048]{2,1,0:T(8,128)(2,1)}, u32[]{:S(2)}, u32[]{:S(2)}) async-start(bf16[8,128,2048]{2,1,0:T(8,128)(2,1)} %bitcast.18), calls=%async_computation.2 | async-start | bytes 8388608 | tf_op jit(solution)/shard_map/all_to_all | solution.py:392
  52.5 33.0 %copy-start.2 = (f32[3,2048]{1,0:T(4,128)S(1)}, f32[3,2048]{1,0:T(4,128)}, u32[]{:S(2)}) copy-start(f32[3,2048]{1,0:T(4,128)} %param.19) | copy-start | bytes 73732
  85.3 103.1 %collective-permute-start = (bf16[8,64,6144]{2,1,0:T(8,128)(2,1)}, bf16[8,64,6144]{2,1,0:T(8,128)(2,1)}, u32[]{:S(2)}, u32[]{:S(2)}) collective-permute-start(bf16[8,64,6144]{2,1,0:T(8,128)(2,1)} %get-tuple-element.31.k_ref.v_ref), channel_id=1, source_target_pairs={{0,1},{1,0},{2,3},{3,2},{4,5},{5,4},{6,7},{7,6},{8,9},{9,8},{10,11... | collective-permute-start | bytes 18874376 | tf_op jit(solution)/shard_map/ppermute | solution.py:416
  428.2 26.9 %collective-permute-start.1 = (bf16[8,64,6144]{2,1,0:T(8,128)(2,1)}, bf16[8,64,6144]{2,1,0:T(8,128)(2,1)}, u32[]{:S(2)}, u32[]{:S(2)}) collective-permute-start(bf16[8,64,6144]{2,1,0:T(8,128)(2,1)} %get-tuple-element.35.k_ref.v_ref), channel_id=1, source_target_pairs={{0,1},{1,0},{2,3},{3,2},{4,5},{5,4},{6,7},{7,6},{8,9},{9,8},{10,11... | collective-permute-start | bytes 18874376 | tf_op jit(solution)/shard_map/ppermute | solution.py:416
  694.8 27.2 %collective-permute-start.2 = (bf16[8,64,6144]{2,1,0:T(8,128)(2,1)}, bf16[8,64,6144]{2,1,0:T(8,128)(2,1)}, u32[]{:S(2)}, u32[]{:S(2)}) collective-permute-start(bf16[8,64,6144]{2,1,0:T(8,128)(2,1)} %get-tuple-element.39.k_ref.v_ref), channel_id=1, source_target_pairs={{0,1},{1,0},{2,3},{3,2},{4,5},{5,4},{6,7},{7,6},{8,9},{9,8},{10,11... | collective-permute-start | bytes 18874376 | tf_op jit(solution)/shard_map/ppermute | solution.py:416
  844.3 59.5 %all-to-all-start.3 = ((bf16[8,128,2048]{2,1,0:T(8,128)(2,1)}), bf16[8,128,2048]{2,1,0:T(8,128)(2,1)}, u32[]{:S(2)}, u32[]{:S(2)}) async-start(bf16[8,128,2048]{2,1,0:T(8,128)(2,1)} %layer_tail.6), calls=%async_computation.3 | async-start | bytes 8388608 | tf_op jit(solution)/shard_map/all_to_all | solution.py:392
